TPU v7x, 32 devices: a whole 2x2x4 slice. The times are simulated.
32 devices in a mesh: field: 2 (over x), ep: 16 (over z, y, core).
Axes of the slice: x: 2, y: 2, z: 4, core: 2. Of those that a mesh axis runs over, the one named last changes fastest.
Arguments:
- images: float32 [64, 16, 256], P(('field', 'ep')), parts along dimension 0, may hold values from -6 to 6
- reference_image: float32 [32, 256], P('field'), parts along dimension 0, may hold values from -6 to 6
- kernels: float32 [16, 23, 23], replicated, may hold values from -0.25 to 0.25
- kernel_index: int32 [64], P(('field', 'ep')), parts along dimension 0, may hold values from 0 to 15
- tile_mask: int32 [64, 16, 2], P(('field', 'ep')), parts along dimension 0, may hold values 0 or 1
- systematics: float32 [64, 40], P('field'), parts along dimension 0, may hold values from -6 to 6
- onsets: int32 [16], P('field'), parts along dimension 0, may hold values from 0 to 27
Outputs:
- coefficients: float32 [48, 32, 256], P(None, ('field', 'ep')), parts along dimension 1
- epoch_scatter: float32 [64], P('field'), parts along dimension 0
There are 2 independent parts, one for each index of `field`. A program takes and returns all parts, laid end to end along the dimension named above; an argument that names none is the same for every part. Nothing has to cross between parts.
All inputs are finite; a program needn't handle non-finite values. No bound on the sum of `tile_mask` on one device may be relied on, other than what follows from the above.
Results may differ from a plain program's by a relative error of at most 0.00011.
Values sent between devices are 32-bit elements; how exact they have to be, the bound alone decides.
A program may use at most 64 MiB of HBM per device.

v0:
```python
import functools

import jax
import jax.numpy as jnp
from jax import lax
from jax.experimental import pallas as pl
from jax.experimental.pallas import tpu as pltpu
from jax.sharding import PartitionSpec as P

cov_ridge = 0.5
fit_ridge = 1.0
LANES = 128
VMEM_GRANT = 24 * 2**20
HIGHEST = lax.Precision.HIGHEST


def dot(a, b, contract):
    return lax.dot_general(
        a, b, ((contract[0], contract[1]), ((), ())), precision=HIGHEST, preferred_element_type=jnp.float32
    )


def iota(shape, axis):
    return lax.broadcasted_iota(jnp.int32, shape, axis)


def exchange_kernel(
    n,
    images_hbm,
    reference_hbm,
    kernels_hbm,
    index_hbm,
    mask_hbm,
    systematics_hbm,
    onsets_hbm,
    pixels,
    total_ref,
    work,
    images_ref,
    reference_ref,
    kernels_ref,
    index_ref,
    mask_ref,
    systematics_ref,
    onsets_ref,
    table,
    table_t,
    taps,
    shifted,
    send,
    recv,
    part,
    parts,
    load_sem,
    send_sem,
    recv_sem,
    part_send_sem,
    part_recv_sem,
):
    local, rows, width = images_ref.shape
    side = kernels_ref.shape[0]
    half = (side - 1) // 2
    tiles = width // LANES
    block = rows // n
    epochs = local * n
    nsys = systematics_ref.shape[1]
    ntr = onsets_ref.shape[0]
    columns = nsys + ntr
    pack = max(LANES // epochs, 1)
    me = lax.axis_index("ep")

    barrier = pltpu.get_barrier_semaphore()
    for d in range(1, n):
        pl.semaphore_signal(
            barrier,
            inc=1,
            device_id={"ep": lax.rem(me + d, n)},
            device_id_type=pl.DeviceIdType.MESH,
        )

    loads = [
        pltpu.make_async_copy(source, target, load_sem.at[i])
        for i, (source, target) in enumerate(
            (
                (index_hbm, index_ref),
                (kernels_hbm, kernels_ref),
                (images_hbm, images_ref),
                (mask_hbm, mask_ref),
                (reference_hbm, reference_ref),
                (systematics_hbm, systematics_ref),
                (onsets_hbm, onsets_ref),
            )
        )
    ]
    for load in loads:
        load.start()
    for load in loads:
        load.wait()

    depth = side * rows
    padded_depth = taps.shape[1]
    lane = iota((rows, LANES), 1)
    column = iota((rows, width), 1)
    for e in range(local):
        table[...] = jnp.zeros_like(table)
        for a in range(side):
            table[a : a + 1, 0:side] = kernels_ref[a, pl.ds(index_ref[e], 1), :]
        table[side + 1 : side + 1 + tiles, 0:rows] = mask_ref[e].astype(jnp.float32)
        table_t[...] = table[...].T
        kept = jnp.where(iota((side, LANES), 1) < side, table_t[0:side, :], 0.0)
        kept = pltpu.roll(kept, LANES - half, axis=1)
        groups = [jnp.zeros((rows, LANES), jnp.float32) for _ in range(padded_depth // LANES)]
        for b in range(side):
            start = b * rows
            at = start % LANES
            row = jnp.broadcast_to(kept[b : b + 1, :], (rows, LANES))
            turned = pltpu.roll(row, at, axis=1, stride=1, stride_axis=0)
            inside = (lane >= at) & (lane < at + rows)
            groups[start // LANES] = jnp.where(inside, turned, groups[start // LANES])
        for g, value in enumerate(groups):
            taps[:, g * LANES : (g + 1) * LANES] = value
        image = images_ref[e]
        for b in range(side):
            move = b - half
            moved = pltpu.roll(image, (-move) % width, axis=1) if move else image
            inside = (column + move >= 0) & (column + move < width)
            shifted[b * rows : (b + 1) * rows, :] = jnp.where(inside, moved, 0.0)
        if padded_depth > depth:
            shifted[depth:, :] = jnp.zeros((padded_depth - depth, width), jnp.float32)
        difference = reference_ref[...] - dot(taps[...], shifted[...], ((1,), (0,)))
        for t in range(tiles):
            good = table_t[0:rows, side + 1 + t : side + 2 + t]
            piece = difference[:, t * LANES : (t + 1) * LANES] * good
            for r in range(rows):
                slot = (r % block) * tiles * local + t * local + e
                send[r // block, slot : slot + 1, :] = piece[r : r + 1, :]

    pl.semaphore_wait(barrier, n - 1)

    def exchange(source, target, send_sems, recv_sems, d):
        return pltpu.make_async_remote_copy(
            src_ref=source,
            dst_ref=target,
            send_sem=send_sems.at[d],
            recv_sem=recv_sems.at[d],
            device_id={"ep": lax.rem(me + d, n)},
            device_id_type=pl.DeviceIdType.MESH,
        )

    for d in (*range(2, n, 2), *range(1, n, 2)):
        exchange(send.at[lax.rem(me + d, n)], recv.at[me], send_sem, recv_sem, d).start()
    recv[me] = send[me]

    work[...] = jnp.zeros_like(work)
    epoch = iota((epochs, LANES), 0).astype(jnp.float32)
    template = iota((epochs, LANES), 1)
    onset = jnp.zeros((epochs, LANES), jnp.float32)
    for k in range(ntr):
        onset = jnp.where(template == k, onsets_ref[k].astype(jnp.float32), onset)
    delays = epoch - onset
    timescale = (template.astype(jnp.float32) + 1.0) * epochs / (2.0 * ntr)
    transient = jnp.where(delays >= 0.0, jnp.exp(-jnp.maximum(delays, 0.0) / timescale), 0.0)
    work[:, epochs : epochs + nsys] = systematics_ref[...]
    work[:, epochs + nsys : epochs + columns] = transient[:, 0:ntr]
    design = work[...]
    outer = dot(design, design, ((1,), (1,)))
    diagonal = iota((epochs, epochs), 0) == iota((epochs, epochs), 1)
    ridge = jnp.where(diagonal, cov_ridge, 0.0)

    for d in range(1, n):
        source = lax.rem(me - d + n, n)
        exchange(send.at[source], recv.at[source], send_sem, recv_sem, d).wait_recv()
    for j in range(n):
        for q in range(block * tiles):
            pixels[j * local : (j + 1) * local, q * LANES : (q + 1) * LANES] = recv[
                j, q * local : (q + 1) * local, :
            ]
    data = pixels[...]

    partial_scatter = dot(data, data, ((1,), (1,)))
    share = epochs // pack
    if pack > 1:
        table[0:epochs, :] = jnp.zeros((epochs, LANES), jnp.float32)
        table[0:epochs, 0:epochs] = partial_scatter
        wide = table[0:epochs, :]
        packed = wide[0:share, :]
        for j in range(1, pack):
            packed = packed + pltpu.roll(wide[j * share : (j + 1) * share, :], j * epochs, axis=1)
        part[...] = packed
    else:
        part[...] = partial_scatter
    for d in (*range(2, n, 2), *range(1, n, 2)):
        exchange(part, parts.at[me], part_send_sem, part_recv_sem, d).start()
    parts[me] = part[...]
    for d in range(1, n):
        source = lax.rem(me - d + n, n)
        exchange(part, parts.at[source], part_send_sem, part_recv_sem, d).wait_recv()
    total = parts[0]
    for j in range(1, n):
        total = total + parts[j]
    total_ref[...] = total
    work[:, 0:epochs] = fit_ridge * outer + ridge
    work[:, epochs + columns : 2 * epochs + columns] = ridge

    for d in range(1, n):
        exchange(send.at[lax.rem(me + d, n)], recv.at[me], send_sem, recv_sem, d).wait_send()
        exchange(part, parts.at[me], part_send_sem, part_recv_sem, d).wait_send()


def fit_kernel(npixels, pixels_ref, total_ref, base_ref, coefficients_ref, epoch_ref, work):
    columns, block, width = coefficients_ref.shape
    epochs = pixels_ref.shape[0]
    pack = epochs // total_ref.shape[0]
    total = total_ref[...]
    if pack > 1:
        pieces = [total] + [
            pltpu.roll(total, LANES - j * epochs, axis=1) for j in range(1, pack)
        ]
        scatter = jnp.concatenate(pieces, axis=0)[:, 0:epochs]
    else:
        scatter = total

    covariance = scatter * (1.0 / npixels)
    work[...] = jnp.zeros_like(work)
    work[:, 0:epochs] = covariance
    work[:, epochs + columns : 2 * epochs + columns] = covariance
    system = work[...] + base_ref[...]
    lanes = system.shape[1]
    group = (8, lanes)
    strips = [system[i : i + 8, :] for i in range(0, epochs, 8)]
    index = iota(group, 0)

    def spread(value, row):
        return jnp.broadcast_to(value[row : row + 1, :], group)

    for home in range(epochs // 8):
        spans = [
            [jnp.broadcast_to(strip[:, k : k + 1], group) for strip in strips]
            for k in range(home * 8, home * 8 + 8)
        ]
        for row in range(0, 8, 2):
            lefts, rights = spans[row], spans[row + 1]
            a, b = spread(lefts[home], row), spread(rights[home], row)
            c, d = spread(lefts[home], row + 1), spread(rights[home], row + 1)
            inverse = 1.0 / (a * d - b * c)

            def step(values):
                first, second = spread(values[home], row), spread(values[home], row + 1)
                upper = (d * first - b * second) * inverse
                lower = (a * second - c * first) * inverse
                values = [
                    v - left * upper - right * lower
                    for v, left, right in zip(values, lefts, rights)
                ]
                values[home] = jnp.where(
                    index == row, upper, jnp.where(index == row + 1, lower, values[home])
                )
                return values

            spans = [step(span) if j > row + 1 else span for j, span in enumerate(spans)]
            strips = step(strips)
    system = jnp.concatenate(strips, axis=0)

    fitted = dot(system, pixels_ref[...], ((0,), (0,)))[epochs : epochs + columns, :]
    for q in range(block):
        coefficients_ref[:, q, :] = fitted[:, q * width : (q + 1) * width]
    product = dot(scatter, system, ((1,), (0,))) * system
    work[0:1, :] = jnp.sum(product, axis=0, keepdims=True) * (1.0 / npixels)
    epoch_ref[...] = work[0, epochs + columns : 2 * epochs + columns]


def ceil_to(value, unit):
    return -(-value // unit) * unit


def solution(mesh):
    n = mesh.shape["ep"]

    def shards(images, reference_image, kernels, kernel_index, tile_mask, systematics, onsets):
        local, rows, width = images.shape
        side = kernels.shape[1]
        tiles = width // LANES
        block = rows // n
        epochs = local * n
        columns = systematics.shape[1] + onsets.shape[0]
        pack = max(LANES // epochs, 1)
        share = epochs // pack
        part_lanes = max(LANES, epochs)
        vmem = pl.BlockSpec(memory_space=pltpu.VMEM)
        dma = pltpu.SemaphoreType.DMA((n,))
        f32 = jnp.float32
        flat_kernels = jnp.transpose(kernels, (1, 0, 2))
        flat_mask = jnp.transpose(tile_mask, (0, 2, 1))
        system_lanes = ceil_to(2 * epochs + columns, LANES)
        pixels, total, base = pl.pallas_call(
            functools.partial(exchange_kernel, n),
            out_shape=(
                jax.ShapeDtypeStruct((epochs, block * width), f32),
                jax.ShapeDtypeStruct((share, part_lanes), f32),
                jax.ShapeDtypeStruct((epochs, system_lanes), f32),
            ),
            in_specs=[pl.BlockSpec(memory_space=pltpu.HBM)] * 7,
            out_specs=(vmem, vmem, vmem),
            scratch_shapes=[
                pltpu.VMEM(images.shape, f32),
                pltpu.VMEM(reference_image.shape, f32),
                pltpu.VMEM(flat_kernels.shape, f32),
                pltpu.SMEM(kernel_index.shape, jnp.int32),
                pltpu.VMEM(flat_mask.shape, jnp.int32),
                pltpu.VMEM(systematics.shape, f32),
                pltpu.SMEM(onsets.shape, jnp.int32),
                pltpu.VMEM((LANES, LANES), f32),
                pltpu.VMEM((LANES, LANES), f32),
                pltpu.VMEM((rows, ceil_to(side * rows, LANES)), f32),
                pltpu.VMEM((ceil_to(side * rows, LANES), width), f32),
                pltpu.VMEM((n, block * tiles * local, LANES), f32),
                pltpu.VMEM((n, block * tiles * local, LANES), f32),
                pltpu.VMEM((share, part_lanes), f32),
                pltpu.VMEM((n, share, part_lanes), f32),
                pltpu.SemaphoreType.DMA((7,)),
                dma,
                dma,
                dma,
                dma,
            ],
            compiler_params=pltpu.CompilerParams(
                collective_id=0, has_side_effects=True, vmem_limit_bytes=VMEM_GRANT
            ),
        )(
            *(
                pltpu.with_memory_space_constraint(value, pltpu.HBM)
                for value in (
                    images,
                    reference_image,
                    flat_kernels,
                    kernel_index,
                    flat_mask,
                    systematics,
                    onsets,
                )
            )
        )
        return pl.pallas_call(
            functools.partial(fit_kernel, float(rows * width)),
            out_shape=(
                jax.ShapeDtypeStruct((columns, block, width), f32),
                jax.ShapeDtypeStruct((epochs,), f32),
            ),
            in_specs=[vmem, vmem, vmem],
            out_specs=(vmem, vmem),
            scratch_shapes=[pltpu.VMEM((epochs, system_lanes), f32)],
            compiler_params=pltpu.CompilerParams(vmem_limit_bytes=VMEM_GRANT),
        )(pixels, total, base)

    in_specs = (
        P(("field", "ep"), None, None),
        P("field", None),
        P(),
        P(("field", "ep")),
        P(("field", "ep"), None, None),
        P("field", None),
        P("field"),
    )
    out_specs = (P(None, ("field", "ep"), None), P("field"))
    return jax.shard_map(shards, mesh=mesh, in_specs=in_specs, out_specs=out_specs, check_vma=False)
```

profile of v0, /device:TPU:0, one launch (start us, length us, event | category | flops | bytes accessed | tf_op | source)
XLA Modules:
  0.0 17.7 jit_solution(6895730538752509322)
XLA Ops:
  0.6 15.2 %shard_map.86 = (f32[32,256]{1,0:T(8,128)S(1)}, f32[8,128]{1,0:T(8,128)S(1)}, f32[32,128]{1,0:T(8,128)S(1)}) custom-call(f32[2,16,256]{2,1,0:T(8,128)} %images_hbm.1, f32[16,256]{1,0:T(8,128)} %reference_hbm.1, f32[23,16,23]{2,1,0:T(8,128)} %bitcast.2, s32[2]{0:T(128)} %index_hbm.1, s32[2,2,16]{2,1,0:T(2,128)} %bitcast.3, f32[32,40]{1,0:T(8,128)} %systematics_hbm.1, ...), custom_call_target="tpu_custom_call" | custom-call | tf_op jit(solution)/shard_map/pallas_call | solution.py:295
  15.8 1.9 %shard_map.87 = (f32[48,1,256]{2,1,0:T(1,128)}, f32[32]{0:T(128)}) custom-call(f32[32,256]{1,0:T(8,128)S(1)} %get-tuple-element.5.pixels_ref, f32[8,128]{1,0:T(8,128)S(1)} %get-tuple-element.6.total_ref, f32[32,128]{1,0:T(8,128)S(1)} %get-tuple-element.7.base_ref), custom_call_target="tpu_custom_call" | custom-call | tf_op jit(solution)/shard_map/pallas_call | solution.py:343
where the time goes:
time: 17.9 us; the launch traced here: 17.7 us
  Pallas kernels  17.1 us (96%)
  between operations  0.64 us (4%)
    pallas_call x1, Pallas kernels, shards(): pl.pallas_call(functools.partial(exchange_kernel, n), out_shape=(jax.Shap...  15.2 us
    pallas_call x1, Pallas kernels, shards(): pl.pallas_call(functools.partial(fit_kernel, float(rows * width)), out_sh...  1.87 us

commit v1 on v0

--- a/solution.py
+++ b/solution.py
@@ -26,6 +26,7 @@
 
 def exchange_kernel(
     n,
+    hubs,
     images_hbm,
     reference_hbm,
     kernels_hbm,
@@ -52,10 +53,12 @@
     part,
     parts,
     load_sem,
-    send_sem,
-    recv_sem,
+    row_sem,
+    hub_sem,
+    part_sem,
+    hub_send_sem,
+    row_send_sem,
     part_send_sem,
-    part_recv_sem,
 ):
     local, rows, width = images_ref.shape
     side = kernels_ref.shape[0]
@@ -68,15 +71,9 @@
     columns = nsys + ntr
     pack = max(LANES // epochs, 1)
     me = lax.axis_index("ep")
-
-    barrier = pltpu.get_barrier_semaphore()
-    for d in range(1, n):
-        pl.semaphore_signal(
-            barrier,
-            inc=1,
-            device_id={"ep": lax.rem(me + d, n)},
-            device_id_type=pl.DeviceIdType.MESH,
-        )
+    count = len(hubs)
+    pieces = recv.shape[0]
+    strips = block * tiles
 
     loads = [
         pltpu.make_async_copy(source, target, load_sem.at[i])
@@ -94,6 +91,15 @@
     ]
     for load in loads:
         load.start()
+
+    barrier = pltpu.get_barrier_semaphore()
+    for d in range(1, n):
+        pl.semaphore_signal(
+            barrier,
+            inc=1,
+            device_id={"ep": lax.rem(me + d, n)},
+            device_id_type=pl.DeviceIdType.MESH,
+        )
     for load in loads:
         load.wait()
 
@@ -131,25 +137,40 @@
         for t in range(tiles):
             good = table_t[0:rows, side + 1 + t : side + 2 + t]
             piece = difference[:, t * LANES : (t + 1) * LANES] * good
-            for r in range(rows):
-                slot = (r % block) * tiles * local + t * local + e
-                send[r // block, slot : slot + 1, :] = piece[r : r + 1, :]
-
+            for r in range(0, rows, 8):
+                first = (r * tiles + t) * local + e
+                send[pl.ds(first, 8, stride=tiles * local), :] = piece[r : r + 8, :]
+
+    sources = send.reshape(rows * tiles, local, LANES)
     pl.semaphore_wait(barrier, n - 1)
 
-    def exchange(source, target, send_sems, recv_sems, d):
+    def copy(source, target, semaphores, device):
+        send_semaphore, semaphore = semaphores
         return pltpu.make_async_remote_copy(
             src_ref=source,
             dst_ref=target,
-            send_sem=send_sems.at[d],
-            recv_sem=recv_sems.at[d],
-            device_id={"ep": lax.rem(me + d, n)},
+            send_sem=send_semaphore,
+            recv_sem=semaphore,
+            device_id={"ep": device},
             device_id_type=pl.DeviceIdType.MESH,
         )
 
-    for d in (*range(2, n, 2), *range(1, n, 2)):
-        exchange(send.at[lax.rem(me + d, n)], recv.at[me], send_sem, recv_sem, d).start()
-    recv[me] = send[me]
+    for k, hub in enumerate(hubs):
+        mine = sources.at[k * pieces : (k + 1) * pieces]
+
+        @pl.when(me != hub)
+        def _():
+            copy(mine, recv.at[:, me], (hub_send_sem, hub_sem), hub).start()
+
+        @pl.when(me == hub)
+        def _():
+            recv[:, me] = mine[...]
+
+    for d in range(1, n):
+        device = lax.rem(me + d, n)
+        rows_of = sources.at[pl.ds(device * strips, strips)]
+        copy(rows_of, pixels.at[:, me], (row_send_sem, row_sem), device).start()
+    pixels[:, me] = sources[pl.ds(me * strips, strips)]
 
     work[...] = jnp.zeros_like(work)
     epoch = iota((epochs, LANES), 0).astype(jnp.float32)
@@ -166,50 +187,88 @@
     outer = dot(design, design, ((1,), (1,)))
     diagonal = iota((epochs, epochs), 0) == iota((epochs, epochs), 1)
     ridge = jnp.where(diagonal, cov_ridge, 0.0)
-
-    for d in range(1, n):
-        source = lax.rem(me - d + n, n)
-        exchange(send.at[source], recv.at[source], send_sem, recv_sem, d).wait_recv()
-    for j in range(n):
-        for q in range(block * tiles):
-            pixels[j * local : (j + 1) * local, q * LANES : (q + 1) * LANES] = recv[
-                j, q * local : (q + 1) * local, :
-            ]
-    data = pixels[...]
-
-    partial_scatter = dot(data, data, ((1,), (1,)))
-    share = epochs // pack
-    if pack > 1:
-        table[0:epochs, :] = jnp.zeros((epochs, LANES), jnp.float32)
-        table[0:epochs, 0:epochs] = partial_scatter
-        wide = table[0:epochs, :]
-        packed = wide[0:share, :]
-        for j in range(1, pack):
-            packed = packed + pltpu.roll(wide[j * share : (j + 1) * share, :], j * epochs, axis=1)
-        part[...] = packed
-    else:
-        part[...] = partial_scatter
-    for d in (*range(2, n, 2), *range(1, n, 2)):
-        exchange(part, parts.at[me], part_send_sem, part_recv_sem, d).start()
-    parts[me] = part[...]
-    for d in range(1, n):
-        source = lax.rem(me - d + n, n)
-        exchange(part, parts.at[source], part_send_sem, part_recv_sem, d).wait_recv()
+    work[:, 0:epochs] = fit_ridge * outer + ridge
+    work[:, epochs + columns : 2 * epochs + columns] = ridge
+
+    def drain(ref, semaphore):
+        pltpu.make_async_copy(ref, ref, semaphore).wait()
+
+    def hub_work(k):
+        others = recv.at[:, 0 : n - 1]
+        drain(others, hub_sem)
+        gathered = recv.reshape(pieces, epochs, LANES)
+        step = min(pieces, 32)
+
+        def gram(start):
+            data = jnp.concatenate([gathered[start + i] for i in range(step)], axis=1)
+            return dot(data, data, ((1,), (1,)))
+
+        if step == pieces:
+            partial_scatter = gram(0)
+        else:
+            partial_scatter = lax.fori_loop(
+                0,
+                pieces // step,
+                lambda i, value: value + gram(i * step),
+                jnp.zeros((epochs, epochs), jnp.float32),
+            )
+        share = epochs // pack
+        if pack > 1:
+            table[0:epochs, :] = jnp.zeros((epochs, LANES), jnp.float32)
+            table[0:epochs, 0:epochs] = partial_scatter
+            wide = table[0:epochs, :]
+            packed = wide[0:share, :]
+            for j in range(1, pack):
+                packed = packed + pltpu.roll(
+                    wide[j * share : (j + 1) * share, :], j * epochs, axis=1
+                )
+            part[...] = packed
+        else:
+            part[...] = partial_scatter
+        for d in range(1, n):
+            device = lax.rem(me + n - d, n)
+            copy(part, parts.at[k], (part_send_sem, part_sem), device).start()
+        parts[k] = part[...]
+
+    for k, hub in enumerate(hubs):
+
+        @pl.when(me == hub)
+        def _():
+            hub_work(k)
+            if count > 1:
+                drain(parts.at[0 : count - 1], part_sem)
+
+    is_hub = functools.reduce(jnp.logical_or, [me == hub for hub in hubs])
+
+    @pl.when(jnp.logical_not(is_hub))
+    def _():
+        drain(parts.at[0:count], part_sem)
+
     total = parts[0]
-    for j in range(1, n):
+    for j in range(1, count):
         total = total + parts[j]
     total_ref[...] = total
-    work[:, 0:epochs] = fit_ridge * outer + ridge
-    work[:, epochs + columns : 2 * epochs + columns] = ridge
-
-    for d in range(1, n):
-        exchange(send.at[lax.rem(me + d, n)], recv.at[me], send_sem, recv_sem, d).wait_send()
-        exchange(part, parts.at[me], part_send_sem, part_recv_sem, d).wait_send()
+    drain(pixels.at[:, 0 : n - 1], row_sem)
+
+    drain(pixels.at[:, 0 : n - 1], row_send_sem)
+
+    @pl.when(jnp.logical_not(is_hub))
+    def _():
+        drain(sources.at[0 : count * pieces], hub_send_sem)
+
+    @pl.when(is_hub)
+    def _():
+        if count > 1:
+            drain(sources.at[0 : (count - 1) * pieces], hub_send_sem)
+        drain(parts.at[0 : n - 1], part_send_sem)
 
 
 def fit_kernel(npixels, pixels_ref, total_ref, base_ref, coefficients_ref, epoch_ref, work):
     columns, block, width = coefficients_ref.shape
-    epochs = pixels_ref.shape[0]
+    strips, n, local, _ = pixels_ref.shape
+    epochs = n * local
+    rows_of = pixels_ref.reshape(strips, epochs, LANES)
+    data = jnp.concatenate([rows_of[i] for i in range(strips)], axis=1)
     pack = epochs // total_ref.shape[0]
     total = total_ref[...]
     if pack > 1:
@@ -261,12 +320,19 @@
             strips = step(strips)
     system = jnp.concatenate(strips, axis=0)
 
-    fitted = dot(system, pixels_ref[...], ((0,), (0,)))[epochs : epochs + columns, :]
+    fitted = dot(system, data, ((0,), (0,)))[epochs : epochs + columns, :]
     for q in range(block):
         coefficients_ref[:, q, :] = fitted[:, q * width : (q + 1) * width]
     product = dot(scatter, system, ((1,), (0,))) * system
     work[0:1, :] = jnp.sum(product, axis=0, keepdims=True) * (1.0 / npixels)
     epoch_ref[...] = work[0, epochs + columns : 2 * epochs + columns]
+
+
+HUBS = (1,)
+
+
+def hub_devices(n):
+    return HUBS
 
 
 def ceil_to(value, unit):
@@ -287,15 +353,18 @@
         share = epochs // pack
         part_lanes = max(LANES, epochs)
         vmem = pl.BlockSpec(memory_space=pltpu.VMEM)
-        dma = pltpu.SemaphoreType.DMA((n,))
+        dma = pltpu.SemaphoreType.DMA
         f32 = jnp.float32
         flat_kernels = jnp.transpose(kernels, (1, 0, 2))
         flat_mask = jnp.transpose(tile_mask, (0, 2, 1))
         system_lanes = ceil_to(2 * epochs + columns, LANES)
+        hubs = hub_devices(n)
+        pieces = rows * tiles // len(hubs)
+        strips = block * tiles
         pixels, total, base = pl.pallas_call(
-            functools.partial(exchange_kernel, n),
+            functools.partial(exchange_kernel, n, hubs),
             out_shape=(
-                jax.ShapeDtypeStruct((epochs, block * width), f32),
+                jax.ShapeDtypeStruct((strips, n, local, LANES), f32),
                 jax.ShapeDtypeStruct((share, part_lanes), f32),
                 jax.ShapeDtypeStruct((epochs, system_lanes), f32),
             ),
@@ -313,11 +382,13 @@
                 pltpu.VMEM((LANES, LANES), f32),
                 pltpu.VMEM((rows, ceil_to(side * rows, LANES)), f32),
                 pltpu.VMEM((ceil_to(side * rows, LANES), width), f32),
-                pltpu.VMEM((n, block * tiles * local, LANES), f32),
-                pltpu.VMEM((n, block * tiles * local, LANES), f32),
+                pltpu.VMEM((rows * tiles * local, LANES), f32),
+                pltpu.VMEM((pieces, n, local, LANES), f32),
                 pltpu.VMEM((share, part_lanes), f32),
                 pltpu.VMEM((n, share, part_lanes), f32),
                 pltpu.SemaphoreType.DMA((7,)),
+                dma,
+                dma,
                 dma,
                 dma,
                 dma,

time: 17.9 us -> 14.8 us (0.83)
  Pallas kernels: 17.1 us -> 14 us
    pallas_call x1, Pallas kernels: 15.2 us -> 12.1 us  [shards(): pl.pallas_call(functools.partial(exchange_kernel, n, hubs), out_shape=(ja...]
where the time goes in v1:
time: 14.8 us; the launch traced here: 14.6 us
  Pallas kernels  14 us (95%)
  between operations  0.64 us (4%)
    pallas_call x1, Pallas kernels, shards(): pl.pallas_call(functools.partial(exchange_kernel, n, hubs), out_shape=(ja...  12.1 us
    pallas_call x1, Pallas kernels, shards(): pl.pallas_call(functools.partial(fit_kernel, float(rows * width)), out_sh...  1.87 us

profile of v1, /device:TPU:0, one launch (start us, length us, event | category | flops | bytes accessed | tf_op | source)
XLA Modules:
  0.0 14.6 jit_solution(8517142926416249592)
XLA Ops:
  0.6 12.1 %shard_map.86 = (f32[2,16,2,128]{3,2,1,0:T(2,128)S(1)}, f32[8,128]{1,0:T(8,128)S(1)}, f32[32,128]{1,0:T(8,128)S(1)}) custom-call(f32[2,16,256]{2,1,0:T(8,128)} %images_hbm.1, f32[16,256]{1,0:T(8,128)} %reference_hbm.1, f32[23,16,23]{2,1,0:T(8,128)} %bitcast.2, s32[2]{0:T(128)} %index_hbm.1, s32[2,2,16]{2,1,0:T(2,128)} %bitcast.3, f32[32,40]{1,0:T(8,128)} %systematics_hbm.1, ...), custom_call_target="tpu_custom_call" | custom-call | tf_op jit(solution)/shard_map/pallas_call | solution.py:364
  12.8 1.9 %shard_map.87 = (f32[48,1,256]{2,1,0:T(1,128)}, f32[32]{0:T(128)}) custom-call(f32[2,16,2,128]{3,2,1,0:T(2,128)S(1)} %get-tuple-element.5.pixels_ref, f32[8,128]{1,0:T(8,128)S(1)} %get-tuple-element.6.total_ref, f32[32,128]{1,0:T(8,128)S(1)} %get-tuple-element.7.base_ref), custom_call_target="tpu_custom_call" | custom-call | tf_op jit(solution)/shard_map/pallas_call | solution.py:414

commit v2 on v1

--- a/solution.py
+++ b/solution.py
@@ -26,7 +26,7 @@
 
 def exchange_kernel(
     n,
-    hubs,
+    hub,
     images_hbm,
     reference_hbm,
     kernels_hbm,
@@ -50,15 +50,15 @@
     shifted,
     send,
     recv,
-    part,
-    parts,
+    spare,
     load_sem,
+    ready_sem,
     row_sem,
     hub_sem,
-    part_sem,
+    total_sem,
     hub_send_sem,
     row_send_sem,
-    part_send_sem,
+    total_send_sem,
 ):
     local, rows, width = images_ref.shape
     side = kernels_ref.shape[0]
@@ -71,7 +71,7 @@
     columns = nsys + ntr
     pack = max(LANES // epochs, 1)
     me = lax.axis_index("ep")
-    count = len(hubs)
+    mate = hub - 1
     pieces = recv.shape[0]
     strips = block * tiles
 
@@ -92,14 +92,22 @@
     for load in loads:
         load.start()
 
+    def signal(semaphore, device):
+        pl.semaphore_signal(
+            semaphore, inc=1, device_id={"ep": device}, device_id_type=pl.DeviceIdType.MESH
+        )
+
     barrier = pltpu.get_barrier_semaphore()
-    for d in range(1, n):
-        pl.semaphore_signal(
-            barrier,
-            inc=1,
-            device_id={"ep": lax.rem(me + d, n)},
-            device_id_type=pl.DeviceIdType.MESH,
-        )
+
+    @pl.when(me == hub)
+    def _():
+        for d in range(1, n):
+            signal(barrier, lax.rem(me + d, n))
+
+    @pl.when(me != hub)
+    def _():
+        signal(barrier, hub)
+
     for load in loads:
         load.wait()
 
@@ -142,35 +150,27 @@
                 send[pl.ds(first, 8, stride=tiles * local), :] = piece[r : r + 8, :]
 
     sources = send.reshape(rows * tiles, local, LANES)
-    pl.semaphore_wait(barrier, n - 1)
-
     def copy(source, target, semaphores, device):
-        send_semaphore, semaphore = semaphores
         return pltpu.make_async_remote_copy(
             src_ref=source,
             dst_ref=target,
-            send_sem=send_semaphore,
-            recv_sem=semaphore,
+            send_sem=semaphores[0],
+            recv_sem=semaphores[1],
             device_id={"ep": device},
             device_id_type=pl.DeviceIdType.MESH,
         )
 
-    for k, hub in enumerate(hubs):
-        mine = sources.at[k * pieces : (k + 1) * pieces]
-
-        @pl.when(me != hub)
-        def _():
-            copy(mine, recv.at[:, me], (hub_send_sem, hub_sem), hub).start()
-
-        @pl.when(me == hub)
-        def _():
-            recv[:, me] = mine[...]
-
-    for d in range(1, n):
-        device = lax.rem(me + d, n)
-        rows_of = sources.at[pl.ds(device * strips, strips)]
-        copy(rows_of, pixels.at[:, me], (row_send_sem, row_sem), device).start()
-    pixels[:, me] = sources[pl.ds(me * strips, strips)]
+    @pl.when(me != hub)
+    def _():
+        pl.semaphore_wait(barrier, 1)
+        copy(sources, recv.at[:, me], (hub_send_sem, hub_sem), hub).start()
+
+    @pl.when(me == hub)
+    def _():
+        pl.semaphore_wait(barrier, n - 1)
+        for d in range(1, n):
+            signal(ready_sem, lax.rem(me + d, n))
+        recv[:, me] = sources[...]
 
     work[...] = jnp.zeros_like(work)
     epoch = iota((epochs, LANES), 0).astype(jnp.float32)
@@ -193,9 +193,25 @@
     def drain(ref, semaphore):
         pltpu.make_async_copy(ref, ref, semaphore).wait()
 
-    def hub_work(k):
-        others = recv.at[:, 0 : n - 1]
-        drain(others, hub_sem)
+    @pl.when(me != hub)
+    def _():
+        pl.semaphore_wait(ready_sem, 1)
+
+    for d in range(n - 2):
+        device = 2 + lax.rem(me + d, n - 2)
+
+        @pl.when(me != device)
+        def _():
+            rows_of = sources.at[pl.ds(device * strips, strips)]
+            copy(rows_of, pixels.at[:, me], (row_send_sem, row_sem), device).start()
+
+    @pl.when(me > hub)
+    def _():
+        pixels[:, me] = sources[pl.ds(me * strips, strips)]
+
+    @pl.when(me == hub)
+    def _():
+        drain(recv.at[:, 0 : n - 1], hub_sem)
         gathered = recv.reshape(pieces, epochs, LANES)
         step = min(pieces, 32)
 
@@ -222,45 +238,34 @@
                 packed = packed + pltpu.roll(
                     wide[j * share : (j + 1) * share, :], j * epochs, axis=1
                 )
-            part[...] = packed
+            total_ref[...] = packed
         else:
-            part[...] = partial_scatter
+            total_ref[...] = partial_scatter
         for d in range(1, n):
             device = lax.rem(me + n - d, n)
-            copy(part, parts.at[k], (part_send_sem, part_sem), device).start()
-        parts[k] = part[...]
-
-    for k, hub in enumerate(hubs):
-
-        @pl.when(me == hub)
-        def _():
-            hub_work(k)
-            if count > 1:
-                drain(parts.at[0 : count - 1], part_sem)
-
-    is_hub = functools.reduce(jnp.logical_or, [me == hub for hub in hubs])
-
-    @pl.when(jnp.logical_not(is_hub))
-    def _():
-        drain(parts.at[0:count], part_sem)
-
-    total = parts[0]
-    for j in range(1, count):
-        total = total + parts[j]
-    total_ref[...] = total
-    drain(pixels.at[:, 0 : n - 1], row_sem)
-
-    drain(pixels.at[:, 0 : n - 1], row_send_sem)
-
-    @pl.when(jnp.logical_not(is_hub))
-    def _():
-        drain(sources.at[0 : count * pieces], hub_send_sem)
-
-    @pl.when(is_hub)
-    def _():
-        if count > 1:
-            drain(sources.at[0 : (count - 1) * pieces], hub_send_sem)
-        drain(parts.at[0 : n - 1], part_send_sem)
+            copy(total_ref, total_ref, (total_send_sem, total_sem), device).start()
+        copy(recv.at[mate * strips : hub * strips], pixels, (row_send_sem, row_sem), mate).start()
+        pixels[...] = recv[hub * strips : (hub + 1) * strips]
+
+    @pl.when(me != hub)
+    def _():
+        drain(total_ref, total_sem)
+        drain(sources, hub_send_sem)
+
+    @pl.when(me == mate)
+    def _():
+        drain(pixels, row_sem)
+        drain(pixels.at[:, 0 : n - 2], row_send_sem)
+
+    @pl.when(me > hub)
+    def _():
+        drain(pixels.at[:, 0 : n - 1], row_sem)
+        drain(pixels.at[:, 0 : n - 3], row_send_sem)
+
+    @pl.when(me == hub)
+    def _():
+        drain(recv.at[0 : 2 * strips, 0 : n - 1], row_send_sem)
+        drain(spare.at[0 : n - 1], total_send_sem)
 
 
 def fit_kernel(npixels, pixels_ref, total_ref, base_ref, coefficients_ref, epoch_ref, work):
@@ -328,11 +333,7 @@
     epoch_ref[...] = work[0, epochs + columns : 2 * epochs + columns]
 
 
-HUBS = (1,)
-
-
-def hub_devices(n):
-    return HUBS
+HUB = 1
 
 
 def ceil_to(value, unit):
@@ -358,11 +359,10 @@
         flat_kernels = jnp.transpose(kernels, (1, 0, 2))
         flat_mask = jnp.transpose(tile_mask, (0, 2, 1))
         system_lanes = ceil_to(2 * epochs + columns, LANES)
-        hubs = hub_devices(n)
-        pieces = rows * tiles // len(hubs)
+        pieces = rows * tiles
         strips = block * tiles
         pixels, total, base = pl.pallas_call(
-            functools.partial(exchange_kernel, n, hubs),
+            functools.partial(exchange_kernel, n, HUB),
             out_shape=(
                 jax.ShapeDtypeStruct((strips, n, local, LANES), f32),
                 jax.ShapeDtypeStruct((share, part_lanes), f32),
@@ -384,9 +384,9 @@
                 pltpu.VMEM((ceil_to(side * rows, LANES), width), f32),
                 pltpu.VMEM((rows * tiles * local, LANES), f32),
                 pltpu.VMEM((pieces, n, local, LANES), f32),
-                pltpu.VMEM((share, part_lanes), f32),
                 pltpu.VMEM((n, share, part_lanes), f32),
                 pltpu.SemaphoreType.DMA((7,)),
+                pltpu.SemaphoreType.REGULAR,
                 dma,
                 dma,
                 dma,

time: 14.8 us -> 13.6 us (0.919)
  Pallas kernels: 14 us -> 12.8 us
    pallas_call x1, Pallas kernels: 12.1 us -> 10.9 us  [shards(): pl.pallas_call(functools.partial(exchange_kernel, n, HUB), out_shape=(jax...]
where the time goes in v2:
time: 13.6 us; the launch traced here: 13.4 us
  Pallas kernels  12.8 us (94%)
  between operations  0.64 us (5%)
    pallas_call x1, Pallas kernels, shards(): pl.pallas_call(functools.partial(exchange_kernel, n, HUB), out_shape=(jax...  10.9 us
    pallas_call x1, Pallas kernels, shards(): pl.pallas_call(functools.partial(fit_kernel, float(rows * width)), out_sh...  1.87 us

profile of v2, /device:TPU:0, one launch (start us, length us, event | category | flops | bytes accessed | tf_op | source)
XLA Modules:
  0.0 13.4 jit_solution(12508374830385612623)
XLA Ops:
  0.6 10.9 %shard_map.86 = (f32[2,16,2,128]{3,2,1,0:T(2,128)S(1)}, f32[8,128]{1,0:T(8,128)S(1)}, f32[32,128]{1,0:T(8,128)S(1)}) custom-call(f32[2,16,256]{2,1,0:T(8,128)} %images_hbm.1, f32[16,256]{1,0:T(8,128)} %reference_hbm.1, f32[23,16,23]{2,1,0:T(8,128)} %bitcast.2, s32[2]{0:T(128)} %index_hbm.1, s32[2,2,16]{2,1,0:T(2,128)} %bitcast.3, f32[32,40]{1,0:T(8,128)} %systematics_hbm.1, ...), custom_call_target="tpu_custom_call" | custom-call | tf_op jit(solution)/shard_map/pallas_call | solution.py:364
  11.5 1.9 %shard_map.87 = (f32[48,1,256]{2,1,0:T(1,128)}, f32[32]{0:T(128)}) custom-call(f32[2,16,2,128]{3,2,1,0:T(2,128)S(1)} %get-tuple-element.5.pixels_ref, f32[8,128]{1,0:T(8,128)S(1)} %get-tuple-element.6.total_ref, f32[32,128]{1,0:T(8,128)S(1)} %get-tuple-element.7.base_ref), custom_call_target="tpu_custom_call" | custom-call | tf_op jit(solution)/shard_map/pallas_call | solution.py:414

commit v3 on v2

v3 whole, which is shorter than its diff:
```python
import functools

import jax
import jax.numpy as jnp
from jax import lax
from jax.experimental import pallas as pl
from jax.experimental.pallas import tpu as pltpu
from jax.sharding import PartitionSpec as P

cov_ridge = 0.5
fit_ridge = 1.0
LANES = 128
GROUP = 8
VMEM_GRANT = 24 * 2**20
HIGHEST = lax.Precision.HIGHEST


def dot(a, b, contract, precision=HIGHEST):
    return lax.dot_general(
        a, b, ((contract[0], contract[1]), ((), ())), precision=precision, preferred_element_type=jnp.float32
    )


def iota(shape, axis):
    return lax.broadcasted_iota(jnp.int32, shape, axis)


def cut(value, count):
    parts = []
    for _ in range(count - 1):
        parts.append(value.astype(jnp.bfloat16))
        value = value - parts[-1].astype(jnp.float32)
    return [*parts, value.astype(jnp.bfloat16)]


def plain_dot(a, b, contract):
    return lax.dot_general(
        a, b, ((contract[0], contract[1]), ((), ())), preferred_element_type=jnp.float32
    )


def turn(value, shift, stride):
    shift %= LANES
    if stride >= 0 and shift + 7 * stride <= LANES:
        return pltpu.roll(value, shift, axis=1, stride=stride, stride_axis=0)
    index = (iota(value.shape, 1) - shift - stride * iota(value.shape, 0)) & (LANES - 1)
    return jnp.take_along_axis(value, index, axis=1)


def exchange_kernel(
    n,
    hub,
    images_hbm,
    reference_hbm,
    kernels_hbm,
    index_hbm,
    mask_hbm,
    systematics_hbm,
    onsets_hbm,
    pixels,
    total_ref,
    work,
    images_ref,
    reference_ref,
    kernels_ref,
    index_ref,
    mask_ref,
    systematics_ref,
    onsets_ref,
    table,
    send,
    recv,
    spare,
    packed_ref,
    load_sem,
    ready_sem,
    row_sem,
    hub_sem,
    total_sem,
    hub_send_sem,
    row_send_sem,
    total_send_sem,
    mate_send_sem,
):
    local, rows, width = images_ref.shape
    side = kernels_hbm.shape[0]
    nk = kernels_hbm.shape[1]
    choices = kernels_ref.reshape(kernels_ref.shape[0] * nk, side)
    half = (side - 1) // 2
    tiles = width // LANES
    block = rows // n
    epochs = local * n
    nsys = systematics_ref.shape[1]
    ntr = onsets_ref.shape[0]
    columns = nsys + ntr
    pack = max(LANES // epochs, 1)
    me = lax.axis_index("ep")
    mate = hub - 1
    pieces = recv.shape[0]
    strips = block * tiles
    share = epochs // pack
    strip = iota((share, total_ref.shape[1]), 1) // epochs

    loads = [
        pltpu.make_async_copy(source, target, load_sem.at[i])
        for i, (source, target) in enumerate(
            (
                (index_hbm, index_ref),
                (kernels_hbm, kernels_ref.at[0:side]),
                (images_hbm, images_ref),
                (mask_hbm, mask_ref),
                (reference_hbm, reference_ref),
                (systematics_hbm, systematics_ref),
                (onsets_hbm, onsets_ref),
            )
        )
    ]
    for load in loads:
        load.start()

    def signal(semaphore, device):
        pl.semaphore_signal(
            semaphore, inc=1, device_id={"ep": device}, device_id_type=pl.DeviceIdType.MESH
        )

    barrier = pltpu.get_barrier_semaphore()

    @pl.when(me == hub)
    def _():
        for d in range(1, n):
            signal(barrier, lax.rem(me + d, n))

    @pl.when(me != hub)
    def _():
        signal(barrier, hub)

    table[...] = jnp.zeros_like(table)
    for load in loads:
        load.wait()

    steps = -(-side // GROUP)
    middle, offset = half // GROUP, half % GROUP
    depth = rows * GROUP
    lane = iota((8, LANES), 1)
    sublane = iota((8, LANES), 0)
    place = lane + sublane - offset
    good = {}
    for e in range(local):
        at = LANES - (e + 1) * 8
        table[at : at + tiles, 0:rows] = mask_ref[e].astype(jnp.float32)
        for t in range(tiles):
            row = jnp.broadcast_to(table[at + t : at + t + 1, :], (8, LANES))
            for r in range(0, rows, 8):
                good[e, t, r] = jnp.take_along_axis(row, sublane + r, axis=1)
    for e in range(local):
        banks = -(-side // 8)
        turned = []
        for g in range(banks):
            table[8 * g : 8 * g + 8, 0:side] = choices[pl.ds(index_ref[e] + 8 * g * nk, 8, stride=nk), :]
            turned.append(
                turn(table[8 * g : 8 * g + 8, :], 8 * g * GROUP, GROUP)
            )
        pages = -(-(GROUP * side + side) // LANES)
        bands = []
        for m in range(steps):
            flat = []
            for page in range(pages):
                total = jnp.zeros((8, LANES), jnp.float32)
                for g in range(banks):
                    low = GROUP * (8 * g + m) - page * LANES
                    if low + 8 * GROUP <= 0 or low >= LANES:
                        continue
                    away = lane - GROUP * sublane - low
                    inside = (away >= 0) & (away < GROUP) & (sublane < side - 8 * g)
                    total = total + jnp.where(inside, turned[g], 0.0)
                flat.append(jnp.broadcast_to(jnp.sum(total, axis=0, keepdims=True), (8, LANES)))
            for h in range(rows // 8):
                pieces_of = []
                for start in range(0, depth, LANES):
                    base = start + GROUP * (half + m - 8 * h)
                    spot = lane + base - GROUP * sublane
                    value = jnp.zeros((8, LANES), jnp.float32)
                    for page in range(pages):
                        if base + LANES <= page * LANES or base - 7 * GROUP >= (page + 1) * LANES:
                            continue
                        moved = turn(flat[page], -base, GROUP)
                        inside = (spot >= page * LANES) & (spot < (page + 1) * LANES)
                        value = jnp.where(inside, moved, value)
                    pieces_of.append(value)
                bands.append(jnp.concatenate(pieces_of, axis=1))
        spread_rows = []
        for r in range(rows):
            moved = [
                turn(
                    jnp.broadcast_to(
                        images_ref[e, r : r + 1, t * LANES : (t + 1) * LANES], (8, LANES)
                    ),
                    offset,
                    -1,
                )
                for t in range(tiles)
            ]
            moved.append(None)
            parts_of = []
            for t in range(tiles + 1):
                value = jnp.zeros((8, LANES), jnp.float32) if moved[t] is None else moved[t]
                before, after = moved[t - 1], moved[(t + 1) % (tiles + 1)]
                value = jnp.where(place < 0, 0.0 if before is None else before, value)
                value = jnp.where(place >= LANES, 0.0 if after is None else after, value)
                parts_of.append(value)
            spread_rows.append(jnp.concatenate(parts_of, axis=1))
        response = dot(
            jnp.concatenate(bands, axis=0),
            jnp.concatenate(spread_rows, axis=0),
            ((1,), (0,)),
            lax.Precision.HIGH,
        )
        span = width + LANES
        model = response[middle * rows : (middle + 1) * rows, 0:width]
        for m in range(steps):
            if m != middle:
                part = response[m * rows : (m + 1) * rows, :]
                model = model + pltpu.roll(part, (-GROUP * (m - middle)) % span, axis=1)[:, 0:width]
        difference = reference_ref[...] - model
        for t in range(tiles):
            for r in range(0, rows, 8):
                first = (r * tiles + t) * local + e
                piece = difference[r : r + 8, t * LANES : (t + 1) * LANES]
                send[pl.ds(first, 8, stride=tiles * local), :] = piece * good[e, t, r]

    sources = send.reshape(rows * tiles, local, LANES)
    def copy(source, target, semaphores, device):
        return pltpu.make_async_remote_copy(
            src_ref=source,
            dst_ref=target,
            send_sem=semaphores[0],
            recv_sem=semaphores[1],
            device_id={"ep": device},
            device_id_type=pl.DeviceIdType.MESH,
        )

    @pl.when(me != hub)
    def _():
        pl.semaphore_wait(barrier, 1)
        copy(sources, recv.at[:, me], (hub_send_sem, hub_sem), hub).start()

    @pl.when(me == hub)
    def _():
        pl.semaphore_wait(barrier, n - 1)
        for d in range(1, n):
            signal(ready_sem, lax.rem(me + d, n))
        recv[:, me] = sources[...]

    work[...] = jnp.zeros_like(work)
    epoch = iota((epochs, LANES), 0).astype(jnp.float32)
    template = iota((epochs, LANES), 1)
    onset = jnp.zeros((epochs, LANES), jnp.float32)
    for k in range(ntr):
        onset = jnp.where(template == k, onsets_ref[k].astype(jnp.float32), onset)
    delays = epoch - onset
    timescale = (template.astype(jnp.float32) + 1.0) * epochs / (2.0 * ntr)
    transient = jnp.where(delays >= 0.0, jnp.exp(-jnp.maximum(delays, 0.0) / timescale), 0.0)
    work[:, epochs : epochs + nsys] = systematics_ref[...]
    work[:, epochs + nsys : epochs + columns] = transient[:, 0:ntr]
    design = work[...]
    outer = dot(design, design, ((1,), (1,)))
    diagonal = iota((epochs, epochs), 0) == iota((epochs, epochs), 1)
    ridge = jnp.where(diagonal, cov_ridge, 0.0)
    lanes = work.shape[1]
    work[:, 0:epochs] = ridge
    work[:, lanes - epochs : lanes] = fit_ridge * outer + ridge

    def drain(ref, semaphore):
        pltpu.make_async_copy(ref, ref, semaphore).wait()

    @pl.when(me != hub)
    def _():
        pl.semaphore_wait(ready_sem, 1)

    for d in range(n - 2):
        device = 2 + lax.rem(me + d, n - 2)

        @pl.when(me != device)
        def _():
            rows_of = sources.at[pl.ds(device * strips, strips)]
            copy(rows_of, pixels.at[:, me], (row_send_sem, row_sem), device).start()

    @pl.when(me > hub)
    def _():
        pixels[:, me] = sources[pl.ds(me * strips, strips)]

    @pl.when(me == hub)
    def _():
        drain(recv.at[:, 0 : n - 1], hub_sem)
        gathered = recv.reshape(pieces, epochs, LANES)
        step = min(pieces, 32)

        def gram(start):
            data = jnp.concatenate([gathered[start + i] for i in range(step)], axis=1)
            both = jnp.concatenate(cut(data, 2), axis=0)
            square = plain_dot(both, both, ((1,), (1,)))
            return square[0:epochs] + square[epochs : 2 * epochs]

        if step == pieces:
            square = gram(0)
        else:
            square = lax.fori_loop(
                0,
                pieces // step,
                lambda i, value: value + gram(i * step),
                jnp.zeros((epochs, 2 * epochs), jnp.float32),
            )
        if pack > 1:
            table[0:epochs, 2 * epochs :] = jnp.zeros((epochs, LANES - 2 * epochs), jnp.float32)
            table[0:epochs, 0 : 2 * epochs] = square
            wide = table[0:epochs, :]
            total = wide
            for j in range(1, pack):
                total = total + pltpu.roll(wide, j * epochs, axis=1)
            total_ref[...] = total
            packed = total[0:share, :]
            for j in range(1, pack):
                packed = jnp.where(strip == j, total[j * share : (j + 1) * share, :], packed)
            packed_ref[...] = packed
        else:
            total_ref[...] = square[:, 0:epochs] + square[:, epochs : 2 * epochs]
        for d in range(1, n):
            device = lax.rem(me + n - d, n)
            if d == 1 and pack > 1:
                copy(total_ref, total_ref, (mate_send_sem, total_sem), device).start()
            elif pack > 1:
                copy(packed_ref, packed_ref, (total_send_sem, total_sem), device).start()
            else:
                copy(total_ref, total_ref, (total_send_sem, total_sem), device).start()
        copy(recv.at[mate * strips : hub * strips], pixels, (row_send_sem, row_sem), mate).start()
        pixels[...] = recv[hub * strips : (hub + 1) * strips]

    @pl.when(me == mate)
    def _():
        drain(total_ref, total_sem)
        drain(sources, hub_send_sem)
        drain(pixels, row_sem)
        drain(pixels.at[:, 0 : n - 2], row_send_sem)

    @pl.when(me > hub)
    def _():
        if pack > 1:
            drain(packed_ref, total_sem)
            packed = packed_ref[...]
            for j in range(pack):
                one = jnp.where(strip == j, packed, 0.0)
                total = one
                for k in range(1, pack):
                    total = total + pltpu.roll(one, k * epochs, axis=1)
                total_ref[j * share : (j + 1) * share, :] = total
        else:
            drain(total_ref, total_sem)
        drain(sources, hub_send_sem)
        drain(pixels.at[:, 0 : n - 1], row_sem)
        drain(pixels.at[:, 0 : n - 3], row_send_sem)

    @pl.when(me == hub)
    def _():
        drain(recv.at[0 : 2 * strips, 0 : n - 1], row_send_sem)
        if pack > 1:
            drain(spare.at[0 : n - 2], total_send_sem)
            drain(total_ref, mate_send_sem)
        else:
            drain(spare.at[0 : n - 1], total_send_sem)


def split_dot(a, b):
    high, middle, low = cut(a, 3)
    left = jnp.concatenate([high, high, middle, high, middle, low], axis=0)
    high, middle, low = cut(b, 3)
    right = jnp.concatenate([high, middle, high, low, middle, high], axis=0)
    return plain_dot(left, right, ((0,), (0,)))


def fit_kernel(npixels, pixels_ref, total_ref, base_ref, coefficients_ref, epoch_ref, work):
    columns, block, width = coefficients_ref.shape
    strips, n, local, _ = pixels_ref.shape
    epochs = n * local
    rows_of = pixels_ref.reshape(strips, epochs, LANES)
    data = jnp.concatenate([rows_of[i] for i in range(strips)], axis=1)
    total = total_ref[...]
    lanes = base_ref.shape[1]
    lane = iota((epochs, lanes), 1)
    covariance = jnp.concatenate([total] * (lanes // total.shape[1]), axis=1) * (1.0 / npixels)
    ends = (lane < epochs) | (lane >= lanes - epochs)
    system = base_ref[...] + jnp.where(ends, covariance, 0.0)
    group = (8, lanes)
    strips = [system[i : i + 8, :] for i in range(0, epochs, 8)]
    index = iota(group, 0)

    def column(value, at):
        tile = at // LANES * LANES
        value = value[:, tile : tile + LANES]
        value = jnp.take_along_axis(value, jnp.full((8, LANES), at - tile, jnp.int32), axis=1)
        return jnp.concatenate([value] * (lanes // LANES), axis=1)

    def spread(value, row):
        return jnp.broadcast_to(value[row : row + 1, :], group)

    for home in range(epochs // 8):
        first_lane = lanes - epochs + home * 8
        spans = [column(strips[home], first_lane + k) for k in range(8)]
        others = [i for i in range(epochs // 8) if i != home]
        factors = {i: [column(strips[i], first_lane + k) for k in range(8)] for i in others}
        value = strips[home]
        for row in range(0, 8, 2):
            left, right = spans[row], spans[row + 1]
            a, b = spread(left, row), spread(right, row)
            c, d = spread(left, row + 1), spread(right, row + 1)
            inverse = 1.0 / (a * d - b * c)

            def step(value):
                first, second = spread(value, row), spread(value, row + 1)
                upper = (d * first - b * second) * inverse
                lower = (a * second - c * first) * inverse
                value = value - left * upper - right * lower
                return jnp.where(index == row, upper, jnp.where(index == row + 1, lower, value))

            spans = [step(span) if j > row + 1 else span for j, span in enumerate(spans)]
            value = step(value)
        strips[home] = value
        pivots = [spread(value, k) for k in range(8)]
        for i in others:
            terms = [factor * pivot for factor, pivot in zip(factors[i], pivots)]
            while len(terms) > 1:
                terms = [p + q for p, q in zip(terms[0::2], terms[1::2])]
            strips[i] = strips[i] - terms[0]
    system = jnp.concatenate(strips, axis=0)

    solved = system[:, 0:LANES] if epochs < LANES else system[:, 0:epochs]
    scatter = total[:, 0:epochs]
    if epochs * 4 == total.shape[1]:
        parts = [part.astype(jnp.float32) for part in cut(total, 3)]
        high, middle, low = parts
        block_of = iota(total.shape, 1) // epochs
        front = jnp.where(block_of == 2, middle, high)
        back = jnp.where(block_of == 0, middle, jnp.where(block_of == 1, low, 0.0))
        left = jnp.concatenate([front, back], axis=1).astype(jnp.bfloat16)
        high, middle, low = cut(solved, 3)
        right = jnp.concatenate([high, middle, high, low, middle, high, high, high], axis=0)
        product = plain_dot(left, right, ((1,), (0,))) * solved
    else:
        product = dot(scatter, solved, ((1,), (0,))) * solved
    epoch_ref[...] = (jnp.sum(product, axis=0, keepdims=True) * (1.0 / npixels))[0, 0:epochs]

    if 6 * epochs <= 256:
        fitted = split_dot(system, data)
    else:
        fitted = dot(system, data, ((0,), (0,)))
    fitted = fitted[epochs : epochs + columns, :]
    for q in range(block):
        coefficients_ref[:, q, :] = fitted[:, q * width : (q + 1) * width]


HUB = 1


def ceil_to(value, unit):
    return -(-value // unit) * unit


def solution(mesh):
    n = mesh.shape["ep"]

    def shards(images, reference_image, kernels, kernel_index, tile_mask, systematics, onsets):
        local, rows, width = images.shape
        side = kernels.shape[1]
        tiles = width // LANES
        block = rows // n
        epochs = local * n
        columns = systematics.shape[1] + onsets.shape[0]
        pack = max(LANES // epochs, 1)
        share = epochs // pack
        part_lanes = max(LANES, epochs)
        vmem = pl.BlockSpec(memory_space=pltpu.VMEM)
        dma = pltpu.SemaphoreType.DMA
        f32 = jnp.float32
        flat_kernels = jnp.transpose(kernels, (1, 0, 2))
        flat_mask = jnp.transpose(tile_mask, (0, 2, 1))
        system_lanes = ceil_to(2 * epochs + columns, LANES)
        pieces = rows * tiles
        strips = block * tiles
        pixels, total, base = pl.pallas_call(
            functools.partial(exchange_kernel, n, HUB),
            out_shape=(
                jax.ShapeDtypeStruct((strips, n, local, LANES), f32),
                jax.ShapeDtypeStruct((epochs, part_lanes), f32),
                jax.ShapeDtypeStruct((epochs, system_lanes), f32),
            ),
            in_specs=[pl.BlockSpec(memory_space=pltpu.HBM)] * 7,
            out_specs=(vmem, vmem, vmem),
            scratch_shapes=[
                pltpu.VMEM(images.shape, f32),
                pltpu.VMEM(reference_image.shape, f32),
                pltpu.VMEM((ceil_to(side, 8), *flat_kernels.shape[1:]), f32),
                pltpu.SMEM(kernel_index.shape, jnp.int32),
                pltpu.VMEM(flat_mask.shape, jnp.int32),
                pltpu.VMEM(systematics.shape, f32),
                pltpu.SMEM(onsets.shape, jnp.int32),
                pltpu.VMEM((LANES, LANES), f32),
                pltpu.VMEM((rows * tiles * local, LANES), f32),
                pltpu.VMEM((pieces, n, local, LANES), f32),
                pltpu.VMEM((n, share, part_lanes), f32),
                pltpu.VMEM((share, part_lanes), f32),
                pltpu.SemaphoreType.DMA((7,)),
                pltpu.SemaphoreType.REGULAR,
                dma,
                dma,
                dma,
                dma,
                dma,
                dma,
                dma,
            ],
            compiler_params=pltpu.CompilerParams(
                collective_id=0, has_side_effects=True, vmem_limit_bytes=VMEM_GRANT
            ),
        )(
            *(
                pltpu.with_memory_space_constraint(value, pltpu.HBM)
                for value in (
                    images,
                    reference_image,
                    flat_kernels,
                    kernel_index,
                    flat_mask,
                    systematics,
                    onsets,
                )
            )
        )
        return pl.pallas_call(
            functools.partial(fit_kernel, float(rows * width)),
            out_shape=(
                jax.ShapeDtypeStruct((columns, block, width), f32),
                jax.ShapeDtypeStruct((epochs,), f32),
            ),
            in_specs=[vmem, vmem, vmem],
            out_specs=(vmem, vmem),
            scratch_shapes=[pltpu.VMEM((epochs, system_lanes), f32)],
            compiler_params=pltpu.CompilerParams(vmem_limit_bytes=VMEM_GRANT),
        )(pixels, total, base)

    in_specs = (
        P(("field", "ep"), None, None),
        P("field", None),
        P(),
        P(("field", "ep")),
        P(("field", "ep"), None, None),
        P("field", None),
        P("field"),
    )
    out_specs = (P(None, ("field", "ep"), None), P("field"))
    return jax.shard_map(shards, mesh=mesh, in_specs=in_specs, out_specs=out_specs, check_vma=False)
```

time: 13.6 us -> 12.9 us (0.949)
  Pallas kernels: 12.8 us -> 12.1 us
    pallas_call x1, Pallas kernels: 10.9 us -> 10.5 us  [shards(): pl.pallas_call(functools.partial(exchange_kernel, n, HUB), out_shape=(jax...]
    pallas_call x1, Pallas kernels: 1.87 us -> 1.57 us  [shards(): pl.pallas_call(functools.partial(fit_kernel, float(rows * width)), out_sh...]
where the time goes in v3:
time: 12.9 us; the launch traced here: 12.7 us
  Pallas kernels  12.1 us (94%)
  between operations  0.64 us (5%)
    pallas_call x1, Pallas kernels, shards(): pl.pallas_call(functools.partial(exchange_kernel, n, HUB), out_shape=(jax...  10.5 us
    pallas_call x1, Pallas kernels, shards(): pl.pallas_call(functools.partial(fit_kernel, float(rows * width)), out_sh...  1.57 us

profile of v3, /device:TPU:0, one launch (start us, length us, event | category | flops | bytes accessed | tf_op | source)
XLA Modules:
  0.0 12.7 jit_solution(12666414748201153829)
XLA Ops:
  0.6 10.5 %shard_map.86 = (f32[2,16,2,128]{3,2,1,0:T(2,128)S(1)}, f32[32,128]{1,0:T(8,128)S(1)}, f32[32,128]{1,0:T(8,128)S(1)}) custom-call(f32[2,16,256]{2,1,0:T(8,128)} %images_hbm.1, f32[16,256]{1,0:T(8,128)} %reference_hbm.1, f32[23,16,23]{2,1,0:T(8,128)} %bitcast.2, s32[2]{0:T(128)} %index_hbm.1, s32[2,2,16]{2,1,0:T(2,128)} %bitcast.3, f32[32,40]{1,0:T(8,128)} %systematics_hbm.1, ...), custom_call_target="tpu_custom_call" | custom-call | tf_op jit(solution)/shard_map/pallas_call | solution.py:488
  11.2 1.6 %shard_map.87 = (f32[48,1,256]{2,1,0:T(1,128)}, f32[32]{0:T(128)}) custom-call(f32[2,16,2,128]{3,2,1,0:T(2,128)S(1)} %get-tuple-element.5.pixels_ref, f32[32,128]{1,0:T(8,128)S(1)} %get-tuple-element.6.total_ref, f32[32,128]{1,0:T(8,128)S(1)} %get-tuple-element.7.base_ref), custom_call_target="tpu_custom_call" | custom-call | tf_op jit(solution)/shard_map/pallas_call | solution.py:537

commit v4 on v3

--- a/solution.py
+++ b/solution.py
@@ -45,6 +45,73 @@
         return pltpu.roll(value, shift, axis=1, stride=stride, stride_axis=0)
     index = (iota(value.shape, 1) - shift - stride * iota(value.shape, 0)) & (LANES - 1)
     return jnp.take_along_axis(value, index, axis=1)
+
+
+def solve(total, base, npixels):
+    epochs, lanes = base.shape
+    lane = iota((epochs, lanes), 1)
+    covariance = jnp.concatenate([total] * (lanes // total.shape[1]), axis=1) * (1.0 / npixels)
+    ends = (lane < epochs) | (lane >= lanes - epochs)
+    system = base + jnp.where(ends, covariance, 0.0)
+    group = (8, lanes)
+    strips = [system[i : i + 8, :] for i in range(0, epochs, 8)]
+    index = iota(group, 0)
+
+    def column(value, at):
+        tile = at // LANES * LANES
+        value = value[:, tile : tile + LANES]
+        value = jnp.take_along_axis(value, jnp.full((8, LANES), at - tile, jnp.int32), axis=1)
+        return jnp.concatenate([value] * (lanes // LANES), axis=1)
+
+    def spread(value, row):
+        return jnp.broadcast_to(value[row : row + 1, :], group)
+
+    def total_of(terms):
+        while len(terms) > 1:
+            terms = [p + q for p, q in zip(terms[0::2], terms[1::2])]
+        return terms[0]
+
+    size = 2 if epochs % 16 == 0 else 1
+    for start in range(0, epochs // 8, size):
+        home = range(start, start + size)
+        order = [i for i in range(epochs // 8) if i not in home]
+        at = lanes - epochs + start * 8
+        spans = [[column(strips[i], at + k) for i in home] for k in range(8 * size)]
+        factors = [[column(strips[i], at + k) for k in range(8 * size)] for i in order]
+        values = [strips[i] for i in home]
+        for first_row in range(0, 8 * size, 2):
+            owner, row = divmod(first_row, 8)
+            lefts, rights = spans[first_row], spans[first_row + 1]
+            a, b = spread(lefts[owner], row), spread(rights[owner], row)
+            c, d = spread(lefts[owner], row + 1), spread(rights[owner], row + 1)
+            inverse = 1.0 / (a * d - b * c)
+            upper, lower = index == row, index == row + 1
+            pair = upper | lower
+            weights = []
+            for i in range(size):
+                one, two = rights[i] * c - lefts[i] * d, lefts[i] * b - rights[i] * a
+                if i == owner:
+                    one = jnp.where(upper, d, jnp.where(lower, -c, one))
+                    two = jnp.where(upper, -b, jnp.where(lower, a, two))
+                weights.append((one * inverse, two * inverse))
+
+            def step(values):
+                first, second = spread(values[owner], row), spread(values[owner], row + 1)
+                return [
+                    (jnp.where(pair, 0.0, value) if i == owner else value)
+                    + weights[i][0] * first
+                    + weights[i][1] * second
+                    for i, value in enumerate(values)
+                ]
+
+            spans = [step(span) if j > first_row + 1 else span for j, span in enumerate(spans)]
+            values = step(values)
+        pivots = [spread(values[k // 8], k % 8) for k in range(8 * size)]
+        for i, factor in zip(order, factors):
+            strips[i] = strips[i] - total_of([p * q for p, q in zip(factor, pivots)])
+        for i, value in zip(home, values):
+            strips[i] = value
+    return jnp.concatenate(strips, axis=0)
 
 
 def exchange_kernel(
@@ -59,7 +126,7 @@
     onsets_hbm,
     pixels,
     total_ref,
-    work,
+    system_ref,
     images_ref,
     reference_ref,
     kernels_ref,
@@ -68,6 +135,7 @@
     systematics_ref,
     onsets_ref,
     table,
+    work,
     send,
     recv,
     spare,
@@ -144,37 +212,46 @@
     lane = iota((8, LANES), 1)
     sublane = iota((8, LANES), 0)
     place = lane + sublane - offset
-    good = {}
+    banks = -(-side // 8)
+    pages = -(-(GROUP * side + side) // LANES)
+    turned = []
     for e in range(local):
-        at = LANES - (e + 1) * 8
-        table[at : at + tiles, 0:rows] = mask_ref[e].astype(jnp.float32)
-        for t in range(tiles):
-            row = jnp.broadcast_to(table[at + t : at + t + 1, :], (8, LANES))
-            for r in range(0, rows, 8):
-                good[e, t, r] = jnp.take_along_axis(row, sublane + r, axis=1)
+        at = e * 8 * banks
+        for g in range(banks):
+            table[at + 8 * g : at + 8 * g + 8, 0:side] = choices[
+                pl.ds(index_ref[e] + 8 * g * nk, 8, stride=nk), :
+            ]
     for e in range(local):
-        banks = -(-side // 8)
-        turned = []
-        for g in range(banks):
-            table[8 * g : 8 * g + 8, 0:side] = choices[pl.ds(index_ref[e] + 8 * g * nk, 8, stride=nk), :]
-            turned.append(
-                turn(table[8 * g : 8 * g + 8, :], 8 * g * GROUP, GROUP)
-            )
-        pages = -(-(GROUP * side + side) // LANES)
-        bands = []
-        for m in range(steps):
-            flat = []
+        at = e * 8 * banks
+        turned.append(
+            [
+                turn(table[at + 8 * g : at + 8 * g + 8, :], 8 * g * GROUP, GROUP)
+                for g in range(banks)
+            ]
+        )
+    windows = {}
+    for m in range(steps):
+        for page in range(pages):
+            for g in range(banks):
+                low = GROUP * (8 * g + m) - page * LANES
+                if low + 8 * GROUP > 0 and low < LANES:
+                    away = lane - GROUP * sublane - low
+                    inside = (away >= 0) & (away < GROUP) & (sublane < side - 8 * g)
+                    windows[m, page, g] = inside
+    flats = {}
+    for m in range(steps):
+        for e in range(local):
             for page in range(pages):
                 total = jnp.zeros((8, LANES), jnp.float32)
                 for g in range(banks):
-                    low = GROUP * (8 * g + m) - page * LANES
-                    if low + 8 * GROUP <= 0 or low >= LANES:
-                        continue
-                    away = lane - GROUP * sublane - low
-                    inside = (away >= 0) & (away < GROUP) & (sublane < side - 8 * g)
-                    total = total + jnp.where(inside, turned[g], 0.0)
-                flat.append(jnp.broadcast_to(jnp.sum(total, axis=0, keepdims=True), (8, LANES)))
-            for h in range(rows // 8):
+                    if (m, page, g) in windows:
+                        total = total + jnp.where(windows[m, page, g], turned[e][g], 0.0)
+                total = jnp.sum(total, axis=0, keepdims=True)
+                flats[e, m, page] = jnp.broadcast_to(total, (8, LANES))
+    bands = [[] for _ in range(local)]
+    for m in range(steps):
+        for h in range(rows // 8):
+            for e in range(local):
                 pieces_of = []
                 for start in range(0, depth, LANES):
                     base = start + GROUP * (half + m - 8 * h)
@@ -183,11 +260,20 @@
                     for page in range(pages):
                         if base + LANES <= page * LANES or base - 7 * GROUP >= (page + 1) * LANES:
                             continue
-                        moved = turn(flat[page], -base, GROUP)
+                        moved = turn(flats[e, m, page], -base, GROUP)
                         inside = (spot >= page * LANES) & (spot < (page + 1) * LANES)
                         value = jnp.where(inside, moved, value)
                     pieces_of.append(value)
-                bands.append(jnp.concatenate(pieces_of, axis=1))
+                bands[e].append(jnp.concatenate(pieces_of, axis=1))
+    good = {}
+    for e in range(local):
+        at = table.shape[0] - (e + 1) * 8
+        table[at : at + tiles, 0:rows] = mask_ref[e].astype(jnp.float32)
+        for t in range(tiles):
+            row = jnp.broadcast_to(table[at + t : at + t + 1, :], (8, LANES))
+            for r in range(0, rows, 8):
+                good[e, t, r] = jnp.take_along_axis(row, sublane + r, axis=1)
+    for e in range(local):
         spread_rows = []
         for r in range(rows):
             moved = [
@@ -210,7 +296,7 @@
                 parts_of.append(value)
             spread_rows.append(jnp.concatenate(parts_of, axis=1))
         response = dot(
-            jnp.concatenate(bands, axis=0),
+            jnp.concatenate(bands[e], axis=0),
             jnp.concatenate(spread_rows, axis=0),
             ((1,), (0,)),
             lax.Precision.HIGH,
@@ -292,6 +378,7 @@
     @pl.when(me == hub)
     def _():
         drain(recv.at[:, 0 : n - 1], hub_sem)
+        copy(recv.at[mate * strips : hub * strips], pixels, (row_send_sem, row_sem), mate).start()
         gathered = recv.reshape(pieces, epochs, LANES)
         step = min(pieces, 32)
 
@@ -332,15 +419,11 @@
                 copy(packed_ref, packed_ref, (total_send_sem, total_sem), device).start()
             else:
                 copy(total_ref, total_ref, (total_send_sem, total_sem), device).start()
-        copy(recv.at[mate * strips : hub * strips], pixels, (row_send_sem, row_sem), mate).start()
         pixels[...] = recv[hub * strips : (hub + 1) * strips]
 
     @pl.when(me == mate)
     def _():
         drain(total_ref, total_sem)
-        drain(sources, hub_send_sem)
-        drain(pixels, row_sem)
-        drain(pixels.at[:, 0 : n - 2], row_send_sem)
 
     @pl.when(me > hub)
     def _():
@@ -355,6 +438,17 @@
                 total_ref[j * share : (j + 1) * share, :] = total
         else:
             drain(total_ref, total_sem)
+
+    system_ref[...] = solve(total_ref[...], work[...], float(rows * width))
+
+    @pl.when(me == mate)
+    def _():
+        drain(sources, hub_send_sem)
+        drain(pixels, row_sem)
+        drain(pixels.at[:, 0 : n - 2], row_send_sem)
+
+    @pl.when(me > hub)
+    def _():
         drain(sources, hub_send_sem)
         drain(pixels.at[:, 0 : n - 1], row_sem)
         drain(pixels.at[:, 0 : n - 3], row_send_sem)
@@ -377,60 +471,14 @@
     return plain_dot(left, right, ((0,), (0,)))
 
 
-def fit_kernel(npixels, pixels_ref, total_ref, base_ref, coefficients_ref, epoch_ref, work):
+def fit_kernel(npixels, pixels_ref, total_ref, system_ref, coefficients_ref, epoch_ref):
     columns, block, width = coefficients_ref.shape
     strips, n, local, _ = pixels_ref.shape
     epochs = n * local
     rows_of = pixels_ref.reshape(strips, epochs, LANES)
     data = jnp.concatenate([rows_of[i] for i in range(strips)], axis=1)
     total = total_ref[...]
-    lanes = base_ref.shape[1]
-    lane = iota((epochs, lanes), 1)
-    covariance = jnp.concatenate([total] * (lanes // total.shape[1]), axis=1) * (1.0 / npixels)
-    ends = (lane < epochs) | (lane >= lanes - epochs)
-    system = base_ref[...] + jnp.where(ends, covariance, 0.0)
-    group = (8, lanes)
-    strips = [system[i : i + 8, :] for i in range(0, epochs, 8)]
-    index = iota(group, 0)
-
-    def column(value, at):
-        tile = at // LANES * LANES
-        value = value[:, tile : tile + LANES]
-        value = jnp.take_along_axis(value, jnp.full((8, LANES), at - tile, jnp.int32), axis=1)
-        return jnp.concatenate([value] * (lanes // LANES), axis=1)
-
-    def spread(value, row):
-        return jnp.broadcast_to(value[row : row + 1, :], group)
-
-    for home in range(epochs // 8):
-        first_lane = lanes - epochs + home * 8
-        spans = [column(strips[home], first_lane + k) for k in range(8)]
-        others = [i for i in range(epochs // 8) if i != home]
-        factors = {i: [column(strips[i], first_lane + k) for k in range(8)] for i in others}
-        value = strips[home]
-        for row in range(0, 8, 2):
-            left, right = spans[row], spans[row + 1]
-            a, b = spread(left, row), spread(right, row)
-            c, d = spread(left, row + 1), spread(right, row + 1)
-            inverse = 1.0 / (a * d - b * c)
-
-            def step(value):
-                first, second = spread(value, row), spread(value, row + 1)
-                upper = (d * first - b * second) * inverse
-                lower = (a * second - c * first) * inverse
-                value = value - left * upper - right * lower
-                return jnp.where(index == row, upper, jnp.where(index == row + 1, lower, value))
-
-            spans = [step(span) if j > row + 1 else span for j, span in enumerate(spans)]
-            value = step(value)
-        strips[home] = value
-        pivots = [spread(value, k) for k in range(8)]
-        for i in others:
-            terms = [factor * pivot for factor, pivot in zip(factors[i], pivots)]
-            while len(terms) > 1:
-                terms = [p + q for p, q in zip(terms[0::2], terms[1::2])]
-            strips[i] = strips[i] - terms[0]
-    system = jnp.concatenate(strips, axis=0)
+    system = system_ref[...]
 
     solved = system[:, 0:LANES] if epochs < LANES else system[:, 0:epochs]
     scatter = total[:, 0:epochs]
@@ -485,7 +533,7 @@
         system_lanes = ceil_to(2 * epochs + columns, LANES)
         pieces = rows * tiles
         strips = block * tiles
-        pixels, total, base = pl.pallas_call(
+        pixels, total, system = pl.pallas_call(
             functools.partial(exchange_kernel, n, HUB),
             out_shape=(
                 jax.ShapeDtypeStruct((strips, n, local, LANES), f32),
@@ -502,7 +550,8 @@
                 pltpu.VMEM(flat_mask.shape, jnp.int32),
                 pltpu.VMEM(systematics.shape, f32),
                 pltpu.SMEM(onsets.shape, jnp.int32),
-                pltpu.VMEM((LANES, LANES), f32),
+                pltpu.VMEM((max(LANES, local * ceil_to(side + 8, 8)), LANES), f32),
+                pltpu.VMEM((epochs, system_lanes), f32),
                 pltpu.VMEM((rows * tiles * local, LANES), f32),
                 pltpu.VMEM((pieces, n, local, LANES), f32),
                 pltpu.VMEM((n, share, part_lanes), f32),
@@ -542,9 +591,8 @@
             ),
             in_specs=[vmem, vmem, vmem],
             out_specs=(vmem, vmem),
-            scratch_shapes=[pltpu.VMEM((epochs, system_lanes), f32)],
             compiler_params=pltpu.CompilerParams(vmem_limit_bytes=VMEM_GRANT),
-        )(pixels, total, base)
+        )(pixels, total, system)
 
     in_specs = (
         P(("field", "ep"), None, None),

time: 12.9 us -> 12.5 us (0.969)
  Pallas kernels: 12.1 us -> 11.7 us
    pallas_call x1, Pallas kernels: 1.57 us -> 0.82 us  [shards(): pl.pallas_call(functools.partial(fit_kernel, float(rows * width)), out_sh...]
    pallas_call x1, Pallas kernels: 10.5 us -> 10.9 us  [shards(): pl.pallas_call(functools.partial(exchange_kernel, n, HUB), out_shape=(jax...]
where the time goes in v4:
time: 12.5 us; the launch traced here: 12.3 us
  Pallas kernels  11.7 us (94%)
  between operations  0.64 us (5%)
    pallas_call x1, Pallas kernels, shards(): pl.pallas_call(functools.partial(exchange_kernel, n, HUB), out_shape=(jax...  10.9 us
    pallas_call x1, Pallas kernels, shards(): pl.pallas_call(functools.partial(fit_kernel, float(rows * width)), out_sh...  0.82 us

profile of v4, /device:TPU:0, one launch (start us, length us, event | category | flops | bytes accessed | tf_op | source)
XLA Modules:
  0.0 12.3 jit_solution(1436839011126065653)
XLA Ops:
  0.6 10.9 %shard_map.86 = (f32[2,16,2,128]{3,2,1,0:T(2,128)S(1)}, f32[32,128]{1,0:T(8,128)S(1)}, f32[32,128]{1,0:T(8,128)S(1)}) custom-call(f32[2,16,256]{2,1,0:T(8,128)} %images_hbm.1, f32[16,256]{1,0:T(8,128)} %reference_hbm.1, f32[23,16,23]{2,1,0:T(8,128)} %bitcast.2, s32[2]{0:T(128)} %index_hbm.1, s32[2,2,16]{2,1,0:T(2,128)} %bitcast.3, f32[32,40]{1,0:T(8,128)} %systematics_hbm.1, ...), custom_call_target="tpu_custom_call" | custom-call | tf_op jit(solution)/shard_map/pallas_call | solution.py:536
  11.5 0.8 %shard_map.87 = (f32[48,1,256]{2,1,0:T(1,128)}, f32[32]{0:T(128)}) custom-call(f32[2,16,2,128]{3,2,1,0:T(2,128)S(1)} %get-tuple-element.5.pixels_ref, f32[32,128]{1,0:T(8,128)S(1)} %get-tuple-element.6.total_ref, f32[32,128]{1,0:T(8,128)S(1)} %get-tuple-element.7.system_ref), custom_call_target="tpu_custom_call" | custom-call | tf_op jit(solution)/shard_map/pallas_call | solution.py:586

commit v5 on v4

--- a/solution.py
+++ b/solution.py
@@ -47,65 +47,95 @@
     return jnp.take_along_axis(value, index, axis=1)
 
 
-def solve(total, base, npixels):
+def spread(value, row):
+    return jnp.broadcast_to(value[row : row + 1, :], value.shape)
+
+
+def column(value, at):
+    lanes = value.shape[1]
+    tile = at // LANES * LANES
+    value = value[:, tile : tile + LANES]
+    value = jnp.take_along_axis(value, jnp.full((8, LANES), at - tile, jnp.int32), axis=1)
+    return jnp.concatenate([value] * (lanes // LANES), axis=1)
+
+
+def total_of(terms):
+    while len(terms) > 1:
+        terms = [p + q for p, q in zip(terms[0::2], terms[1::2])]
+    return terms[0]
+
+
+def eliminate(values, at):
+    size = len(values)
+    index = iota(values[0].shape, 0)
+    spans = [[column(value, at + k) for value in values] for k in range(8 * size)]
+    for first_row in range(0, 8 * size, 2):
+        owner, row = divmod(first_row, 8)
+        lefts, rights = spans[first_row], spans[first_row + 1]
+        a, b = spread(lefts[owner], row), spread(rights[owner], row)
+        c, d = spread(lefts[owner], row + 1), spread(rights[owner], row + 1)
+        inverse = 1.0 / (a * d - b * c)
+        upper, lower = index == row, index == row + 1
+        pair = upper | lower
+        weights = []
+        for i in range(size):
+            one, two = rights[i] * c - lefts[i] * d, lefts[i] * b - rights[i] * a
+            if i == owner:
+                one = jnp.where(upper, d, jnp.where(lower, -c, one))
+                two = jnp.where(upper, -b, jnp.where(lower, a, two))
+            weights.append((one * inverse, two * inverse))
+
+        def step(values):
+            first, second = spread(values[owner], row), spread(values[owner], row + 1)
+            return [
+                (jnp.where(pair, 0.0, value) if i == owner else value)
+                + weights[i][0] * first
+                + weights[i][1] * second
+                for i, value in enumerate(values)
+            ]
+
+        spans = [step(span) if j > first_row + 1 else span for j, span in enumerate(spans)]
+        values = step(values)
+    return values
+
+
+def invert_early(square, base, npixels, inverse_ref):
+    count, lanes = square.shape
+    epochs = base.shape[0]
+    lane = iota((count, lanes), 1)
+    matrix = (square + pltpu.roll(square, lanes - count, axis=1)) * (1.0 / npixels)
+    matrix = matrix + pltpu.roll(base[0:count, :], epochs, axis=1)
+    unit = jnp.where(lane - count == iota((count, lanes), 0), 1.0, 0.0)
+    system = jnp.where(lane < count, matrix, unit)
+    values = eliminate([system[i : i + 8, :] for i in range(0, count, 8)], 0)
+    for i, value in enumerate(values):
+        for k in range(count):
+            inverse_ref[i * count + k] = column(value, count + k)
+
+
+def solve(total, base, npixels, inverse_ref):
     epochs, lanes = base.shape
     lane = iota((epochs, lanes), 1)
     covariance = jnp.concatenate([total] * (lanes // total.shape[1]), axis=1) * (1.0 / npixels)
     ends = (lane < epochs) | (lane >= lanes - epochs)
     system = base + jnp.where(ends, covariance, 0.0)
-    group = (8, lanes)
     strips = [system[i : i + 8, :] for i in range(0, epochs, 8)]
-    index = iota(group, 0)
-
-    def column(value, at):
-        tile = at // LANES * LANES
-        value = value[:, tile : tile + LANES]
-        value = jnp.take_along_axis(value, jnp.full((8, LANES), at - tile, jnp.int32), axis=1)
-        return jnp.concatenate([value] * (lanes // LANES), axis=1)
-
-    def spread(value, row):
-        return jnp.broadcast_to(value[row : row + 1, :], group)
-
-    def total_of(terms):
-        while len(terms) > 1:
-            terms = [p + q for p, q in zip(terms[0::2], terms[1::2])]
-        return terms[0]
-
     size = 2 if epochs % 16 == 0 else 1
     for start in range(0, epochs // 8, size):
         home = range(start, start + size)
         order = [i for i in range(epochs // 8) if i not in home]
         at = lanes - epochs + start * 8
-        spans = [[column(strips[i], at + k) for i in home] for k in range(8 * size)]
         factors = [[column(strips[i], at + k) for k in range(8 * size)] for i in order]
         values = [strips[i] for i in home]
-        for first_row in range(0, 8 * size, 2):
-            owner, row = divmod(first_row, 8)
-            lefts, rights = spans[first_row], spans[first_row + 1]
-            a, b = spread(lefts[owner], row), spread(rights[owner], row)
-            c, d = spread(lefts[owner], row + 1), spread(rights[owner], row + 1)
-            inverse = 1.0 / (a * d - b * c)
-            upper, lower = index == row, index == row + 1
-            pair = upper | lower
-            weights = []
-            for i in range(size):
-                one, two = rights[i] * c - lefts[i] * d, lefts[i] * b - rights[i] * a
-                if i == owner:
-                    one = jnp.where(upper, d, jnp.where(lower, -c, one))
-                    two = jnp.where(upper, -b, jnp.where(lower, a, two))
-                weights.append((one * inverse, two * inverse))
-
-            def step(values):
-                first, second = spread(values[owner], row), spread(values[owner], row + 1)
-                return [
-                    (jnp.where(pair, 0.0, value) if i == owner else value)
-                    + weights[i][0] * first
-                    + weights[i][1] * second
-                    for i, value in enumerate(values)
-                ]
-
-            spans = [step(span) if j > first_row + 1 else span for j, span in enumerate(spans)]
-            values = step(values)
+        if inverse_ref is not None and start == 0:
+            count = 8 * size
+            pivots = [spread(values[k // 8], k % 8) for k in range(count)]
+            values = [
+                total_of([inverse_ref[i * count + k] * pivots[k] for k in range(count)])
+                for i in range(size)
+            ]
+        else:
+            values = eliminate(values, at)
         pivots = [spread(values[k // 8], k % 8) for k in range(8 * size)]
         for i, factor in zip(order, factors):
             strips[i] = strips[i] - total_of([p * q for p, q in zip(factor, pivots)])
@@ -140,11 +170,15 @@
     recv,
     spare,
     packed_ref,
+    early_ref,
+    inverse_ref,
     load_sem,
     ready_sem,
     row_sem,
     hub_sem,
     total_sem,
+    early_sem,
+    early_send_sem,
     hub_send_sem,
     row_send_sem,
     total_send_sem,
@@ -328,7 +362,7 @@
     @pl.when(me != hub)
     def _():
         pl.semaphore_wait(barrier, 1)
-        copy(sources, recv.at[:, me], (hub_send_sem, hub_sem), hub).start()
+        copy(sources, recv.at[:, me], (hub_send_sem, hub_sem.at[me // (n // 2)]), hub).start()
 
     @pl.when(me == hub)
     def _():
@@ -375,11 +409,35 @@
     def _():
         pixels[:, me] = sources[pl.ds(me * strips, strips)]
 
+    count = early_ref.shape[0]
+    early = count * 2 == epochs
+    gathered = recv.reshape(pieces, epochs, LANES)
+
     @pl.when(me == hub)
     def _():
-        drain(recv.at[:, 0 : n - 1], hub_sem)
+        drain(recv.at[:, 0 : n // 2 - 1], hub_sem.at[0])
+        if early:
+            data = jnp.concatenate([gathered[i, 0:count, :] for i in range(pieces)], axis=1)
+            both = jnp.concatenate(cut(data, 2), axis=0)
+            square = plain_dot(both, both, ((1,), (1,)))
+            early_ref[...] = jnp.zeros_like(early_ref)
+            early_ref[:, 0 : 2 * count] = square[0:count] + square[count : 2 * count]
+            for d in range(1, n):
+                device = lax.rem(me + n - d, n)
+                copy(early_ref, early_ref, (early_send_sem, early_sem), device).start()
+
+    if early:
+
+        @pl.when(me != hub)
+        def _():
+            drain(early_ref, early_sem)
+
+        invert_early(early_ref[...], work[...], float(rows * width), inverse_ref)
+
+    @pl.when(me == hub)
+    def _():
+        drain(recv.at[:, 0 : n // 2], hub_sem.at[1])
         copy(recv.at[mate * strips : hub * strips], pixels, (row_send_sem, row_sem), mate).start()
-        gathered = recv.reshape(pieces, epochs, LANES)
         step = min(pieces, 32)
 
         def gram(start):
@@ -439,7 +497,9 @@
         else:
             drain(total_ref, total_sem)
 
-    system_ref[...] = solve(total_ref[...], work[...], float(rows * width))
+    system_ref[...] = solve(
+        total_ref[...], work[...], float(rows * width), inverse_ref if early else None
+    )
 
     @pl.when(me == mate)
     def _():
@@ -456,6 +516,8 @@
     @pl.when(me == hub)
     def _():
         drain(recv.at[0 : 2 * strips, 0 : n - 1], row_send_sem)
+        if early:
+            drain(recv.at[0 : count // local, 0 : n - 1], early_send_sem)
         if pack > 1:
             drain(spare.at[0 : n - 2], total_send_sem)
             drain(total_ref, mate_send_sem)
@@ -506,6 +568,7 @@
 
 
 HUB = 1
+EARLY = 16
 
 
 def ceil_to(value, unit):
@@ -556,8 +619,12 @@
                 pltpu.VMEM((pieces, n, local, LANES), f32),
                 pltpu.VMEM((n, share, part_lanes), f32),
                 pltpu.VMEM((share, part_lanes), f32),
+                pltpu.VMEM((EARLY, LANES), f32),
+                pltpu.VMEM((2 * EARLY, 8, LANES), f32),
                 pltpu.SemaphoreType.DMA((7,)),
                 pltpu.SemaphoreType.REGULAR,
+                dma,
+                pltpu.SemaphoreType.DMA((2,)),
                 dma,
                 dma,
                 dma,

time: 12.5 us -> 12.4 us (level)
  no operation moved by 1% of the time
where the time goes in v5:
time: 12.4 us; the launch traced here: 12.2 us
  Pallas kernels  11.6 us (94%)
  between operations  0.64 us (5%)
    pallas_call x1, Pallas kernels, shards(): pl.pallas_call(functools.partial(exchange_kernel, n, HUB), out_shape=(jax...  10.8 us
    pallas_call x1, Pallas kernels, shards(): pl.pallas_call(functools.partial(fit_kernel, float(rows * width)), out_sh...  0.82 us

profile of v5, /device:TPU:0, one launch (start us, length us, event | category | flops | bytes accessed | tf_op | source)
XLA Modules:
  0.0 12.2 jit_solution(5223346400184807744)
XLA Ops:
  0.6 10.8 %shard_map.86 = (f32[2,16,2,128]{3,2,1,0:T(2,128)S(1)}, f32[32,128]{1,0:T(8,128)S(1)}, f32[32,128]{1,0:T(8,128)S(1)}) custom-call(f32[2,16,256]{2,1,0:T(8,128)} %images_hbm.1, f32[16,256]{1,0:T(8,128)} %reference_hbm.1, f32[23,16,23]{2,1,0:T(8,128)} %bitcast.2, s32[2]{0:T(128)} %index_hbm.1, s32[2,2,16]{2,1,0:T(2,128)} %bitcast.3, f32[32,40]{1,0:T(8,128)} %systematics_hbm.1, ...), custom_call_target="tpu_custom_call" | custom-call | tf_op jit(solution)/shard_map/pallas_call | solution.py:599
  11.4 0.8 %shard_map.87 = (f32[48,1,256]{2,1,0:T(1,128)}, f32[32]{0:T(128)}) custom-call(f32[2,16,2,128]{3,2,1,0:T(2,128)S(1)} %get-tuple-element.5.pixels_ref, f32[32,128]{1,0:T(8,128)S(1)} %get-tuple-element.6.total_ref, f32[32,128]{1,0:T(8,128)S(1)} %get-tuple-element.7.system_ref), custom_call_target="tpu_custom_call" | custom-call | tf_op jit(solution)/shard_map/pallas_call | solution.py:653

commit v6 on v5

--- a/solution.py
+++ b/solution.py
@@ -178,11 +178,6 @@
     hub_sem,
     total_sem,
     early_sem,
-    early_send_sem,
-    hub_send_sem,
-    row_send_sem,
-    total_send_sem,
-    mate_send_sem,
 ):
     local, rows, width = images_ref.shape
     side = kernels_hbm.shape[0]
@@ -197,6 +192,9 @@
     columns = nsys + ntr
     pack = max(LANES // epochs, 1)
     me = lax.axis_index("ep")
+    hub_send_sem, row_send_sem, total_send_sem, mate_send_sem, early_send_sem = (
+        load_sem.at[i] for i in range(5)
+    )
     mate = hub - 1
     pieces = recv.shape[0]
     strips = block * tiles
@@ -627,11 +625,6 @@
                 pltpu.SemaphoreType.DMA((2,)),
                 dma,
                 dma,
-                dma,
-                dma,
-                dma,
-                dma,
-                dma,
             ],
             compiler_params=pltpu.CompilerParams(
                 collective_id=0, has_side_effects=True, vmem_limit_bytes=VMEM_GRANT

time: 12.4 us -> 12.4 us (level)
  no operation moved by 1% of the time
where the time goes in v6:
time: 12.4 us; the launch traced here: 12.2 us
  Pallas kernels  11.6 us (94%)
  between operations  0.64 us (5%)
    pallas_call x1, Pallas kernels, shards(): pl.pallas_call(functools.partial(exchange_kernel, n, HUB), out_shape=(jax...  10.7 us
    pallas_call x1, Pallas kernels, shards(): pl.pallas_call(functools.partial(fit_kernel, float(rows * width)), out_sh...  0.82 us

profile of v6, /device:TPU:0, one launch (start us, length us, event | category | flops | bytes accessed | tf_op | source)
XLA Modules:
  0.0 12.2 jit_solution(7869949139847141981)
XLA Ops:
  0.6 10.7 %shard_map.86 = (f32[2,16,2,128]{3,2,1,0:T(2,128)S(1)}, f32[32,128]{1,0:T(8,128)S(1)}, f32[32,128]{1,0:T(8,128)S(1)}) custom-call(f32[2,16,256]{2,1,0:T(8,128)} %images_hbm.1, f32[16,256]{1,0:T(8,128)} %reference_hbm.1, f32[23,16,23]{2,1,0:T(8,128)} %bitcast.2, s32[2]{0:T(128)} %index_hbm.1, s32[2,2,16]{2,1,0:T(2,128)} %bitcast.3, f32[32,40]{1,0:T(8,128)} %systematics_hbm.1, ...), custom_call_target="tpu_custom_call" | custom-call | tf_op jit(solution)/shard_map/pallas_call | solution.py:597
  11.4 0.8 %shard_map.87 = (f32[48,1,256]{2,1,0:T(1,128)}, f32[32]{0:T(128)}) custom-call(f32[2,16,2,128]{3,2,1,0:T(2,128)S(1)} %get-tuple-element.5.pixels_ref, f32[32,128]{1,0:T(8,128)S(1)} %get-tuple-element.6.total_ref, f32[32,128]{1,0:T(8,128)S(1)} %get-tuple-element.7.system_ref), custom_call_target="tpu_custom_call" | custom-call | tf_op jit(solution)/shard_map/pallas_call | solution.py:646

commit v7 on v6

--- a/solution.py
+++ b/solution.py
@@ -524,10 +524,10 @@
 
 
 def split_dot(a, b):
-    high, middle, low = cut(a, 3)
-    left = jnp.concatenate([high, high, middle, high, middle, low], axis=0)
-    high, middle, low = cut(b, 3)
-    right = jnp.concatenate([high, middle, high, low, middle, high], axis=0)
+    high, low = cut(a, 2)
+    left = jnp.concatenate([high, high, low, low], axis=0)
+    high, low = cut(b, 2)
+    right = jnp.concatenate([high, low, high, low], axis=0)
     return plain_dot(left, right, ((0,), (0,)))
 
 
@@ -543,20 +543,17 @@
     solved = system[:, 0:LANES] if epochs < LANES else system[:, 0:epochs]
     scatter = total[:, 0:epochs]
     if epochs * 4 == total.shape[1]:
-        parts = [part.astype(jnp.float32) for part in cut(total, 3)]
-        high, middle, low = parts
+        high, low = (part.astype(jnp.float32) for part in cut(total, 2))
         block_of = iota(total.shape, 1) // epochs
-        front = jnp.where(block_of == 2, middle, high)
-        back = jnp.where(block_of == 0, middle, jnp.where(block_of == 1, low, 0.0))
-        left = jnp.concatenate([front, back], axis=1).astype(jnp.bfloat16)
-        high, middle, low = cut(solved, 3)
-        right = jnp.concatenate([high, middle, high, low, middle, high, high, high], axis=0)
+        left = jnp.where(block_of < 2, high, low).astype(jnp.bfloat16)
+        high, low = cut(solved, 2)
+        right = jnp.concatenate([high, low, high, low], axis=0)
         product = plain_dot(left, right, ((1,), (0,))) * solved
     else:
         product = dot(scatter, solved, ((1,), (0,))) * solved
     epoch_ref[...] = (jnp.sum(product, axis=0, keepdims=True) * (1.0 / npixels))[0, 0:epochs]
 
-    if 6 * epochs <= 256:
+    if 4 * epochs <= 256:
         fitted = split_dot(system, data)
     else:
         fitted = dot(system, data, ((0,), (0,)))

time: 12.4 us -> 12.3 us (level)
  no operation moved by 1% of the time
where the time goes in v7:
time: 12.3 us; the launch traced here: 12.2 us
  Pallas kernels  11.6 us (94%)
  between operations  0.64 us (5%)
    pallas_call x1, Pallas kernels, shards(): pl.pallas_call(functools.partial(exchange_kernel, n, HUB), out_shape=(jax...  10.7 us
    pallas_call x1, Pallas kernels, shards(): pl.pallas_call(functools.partial(fit_kernel, float(rows * width)), out_sh...  0.82 us

profile of v7, /device:TPU:0, one launch (start us, length us, event | category | flops | bytes accessed | tf_op | source)
XLA Modules:
  0.0 12.2 jit_solution(12024102086705876393)
XLA Ops:
  0.6 10.7 %shard_map.86 = (f32[2,16,2,128]{3,2,1,0:T(2,128)S(1)}, f32[32,128]{1,0:T(8,128)S(1)}, f32[32,128]{1,0:T(8,128)S(1)}) custom-call(f32[2,16,256]{2,1,0:T(8,128)} %images_hbm.1, f32[16,256]{1,0:T(8,128)} %reference_hbm.1, f32[23,16,23]{2,1,0:T(8,128)} %bitcast.2, s32[2]{0:T(128)} %index_hbm.1, s32[2,2,16]{2,1,0:T(2,128)} %bitcast.3, f32[32,40]{1,0:T(8,128)} %systematics_hbm.1, ...), custom_call_target="tpu_custom_call" | custom-call | tf_op jit(solution)/shard_map/pallas_call | solution.py:594
  11.4 0.8 %shard_map.87 = (f32[48,1,256]{2,1,0:T(1,128)}, f32[32]{0:T(128)}) custom-call(f32[2,16,2,128]{3,2,1,0:T(2,128)S(1)} %get-tuple-element.5.pixels_ref, f32[32,128]{1,0:T(8,128)S(1)} %get-tuple-element.6.total_ref, f32[32,128]{1,0:T(8,128)S(1)} %get-tuple-element.7.system_ref), custom_call_target="tpu_custom_call" | custom-call | tf_op jit(solution)/shard_map/pallas_call | solution.py:643
